TPU v7x, 128 devices: a whole 4x4x4 slice. The times are simulated.
128 devices in a mesh: task: 2 (over z_lo), batch: 64 (over y, z_hi, x, core).
Axes of the slice: x: 4, y: 4, z: 4 (z_hi: 2, z_lo: 2; z = z_hi * 2 + z_lo), core: 2. Of those that a mesh axis runs over, the one named last changes fastest.
Arguments:
- pooled: bfloat16 [49152, 3328], P('batch'), may hold values from -6 to 6
- gate_weight: bfloat16 [3328, 8, 4], P(None, 'task'), may hold values from -0.21875 to 0.21875
- w_first: bfloat16 [8, 3328, 1024], P('task', 'batch'), may hold values from -0.15625 to 0.15625
- w_second: bfloat16 [8, 1024, 512], P('task', 'batch'), may hold values from -0.25 to 0.25
- w_third: bfloat16 [8, 512, 256], P('task', 'batch'), may hold values from -0.375 to 0.375
- tower_hidden: bfloat16 [4, 256, 128], P('task'), may hold values from -0.5 to 0.5
- tower_out: bfloat16 [4, 128], P('task'), may hold values from -0.75 to 0.75
Outputs:
- task_logits: float32 [49152, 4], P('batch', 'task')
All inputs are finite; a program needn't handle non-finite values.
Results may differ from a plain program's by a relative error of at most 0.02.
Values may be sent and summed in bfloat16 or wider, within the bound.
A program may use at most 128 MiB of HBM per device.

v0:
```python
import jax
import jax.numpy as jnp
from jax import lax
from jax.sharding import Mesh
from jax.sharding import PartitionSpec as P

BATCH = ("batch_0", "batch_1", "batch_2", "batch_3")


def sent_to_all(shard, axis):
    count = lax.axis_size(axis)
    return lax.all_to_all(
        jnp.broadcast_to(shard[None], (count, *shard.shape)), axis, 0, 0, tiled=True
    )


def laid_out(parts, dim):
    parts = jnp.moveaxis(parts, 0, dim)
    shape = parts.shape
    return parts.reshape(*shape[:dim], shape[dim] * shape[dim + 1], *shape[dim + 2 :])


def whole_of(shard, axes, dim):
    far, near = axes
    parts = sent_to_all(sent_to_all(shard, far), near)
    return laid_out(parts.swapaxes(0, 1).reshape(-1, *shard.shape), dim)


def gather_directly(shard, axis, dim):
    return laid_out(sent_to_all(shard, axis), dim)


def in_blocks(shard, dim, count):
    before, after = (shard.shape[:dim], shard.shape[dim + 1 :])
    return jnp.moveaxis(shard.reshape(*before, count, -1, *after), dim, 0)


def sent_and_summed(shard, axis, dim):
    count = lax.axis_size(axis)
    parts = lax.all_to_all(in_blocks(shard, dim, count), axis, 0, 0, tiled=True)
    return jnp.sum(parts.astype(jnp.float32), axis=0)


def sent_together(arrays, axis, dim, along):
    columns = [a.reshape(*a.shape[:along], -1) for a in arrays]
    both = jnp.concatenate(columns, axis=along)
    out, at, outs = (sent_and_summed(both, axis, dim), 0, [])
    for a, column in zip(arrays, columns):
        section = out[..., at : at + column.shape[along]]
        outs.append(section.reshape(*section.shape[:along], *a.shape[along:]))
        at += column.shape[along]
    return tuple(outs)


def per_device(pooled, gate_weight, w_first, w_second, w_third, tower_hidden, tower_out):
    tok_rows = pooled.shape[0]
    width_in = pooled.shape[1]
    local_experts = w_first.shape[0]
    all_tasks = gate_weight.shape[2]
    gathered = lax.all_gather(w_first, BATCH, axis=1, tiled=True)
    summed = jnp.einsum("tr,erh->eth", pooled, gathered, preferred_element_type=jnp.float32)
    first = jax.nn.relu(summed).astype(jnp.bfloat16)
    logits = jnp.dot(
        pooled,
        gate_weight.reshape(width_in, local_experts * all_tasks),
        preferred_element_type=jnp.float32,
    )
    weights = jnp.exp(logits.reshape(tok_rows, local_experts, all_tasks))
    gate_total = jnp.sum(weights, axis=1)
    columns = first
    second = jax.nn.relu(
        jnp.einsum(
            "etr,erh->eth",
            columns,
            whole_of(w_second, (("batch_0", "batch_1", "batch_2"), "batch_3"), 1),
            preferred_element_type=jnp.float32,
        )
    ).astype(jnp.bfloat16)
    columns = second
    expert_out = jax.nn.relu(
        jnp.einsum(
            "etr,erh->eth",
            columns,
            gather_directly(w_third, BATCH, 1),
            preferred_element_type=jnp.float32,
        )
    ).astype(jnp.bfloat16)
    numer = jnp.einsum("tek,eth->tkh", weights, expert_out.astype(jnp.float32))
    numer_own, total_own = sent_together(
        (numer.astype(jnp.bfloat16), gate_total.astype(jnp.bfloat16)), "task", 1, 2
    )
    mix = (numer_own / total_own[:, :, None]).astype(jnp.bfloat16)
    tower = jax.nn.relu(
        jnp.einsum("tkh,khm->tkm", mix, tower_hidden, preferred_element_type=jnp.float32)
    ).astype(jnp.bfloat16)
    return jnp.einsum("tkm,km->tk", tower, tower_out, preferred_element_type=jnp.float32)


def solution(mesh):
    torus = Mesh(
        mesh.devices.reshape(mesh.shape["task"], 4, 2, 4, 2),
        ("task", "batch_0", "batch_1", "batch_2", "batch_3"),
    )
    return jax.shard_map(
        per_device,
        mesh=torus,
        in_specs=(
            P(BATCH, None),
            P(None, "task", None),
            P("task", BATCH, None),
            P("task", BATCH, None),
            P("task", BATCH, None),
            P("task", None, None),
            P("task", None),
        ),
        out_specs=P(BATCH, "task"),
        check_vma=False,
    )
```

profile of v0, /device:TPU:1, one launch (start us, length us, event | category | flops | bytes accessed | tf_op | source)
XLA Modules:
  0.0 262.6 jit_solution(3409907024084727435)
XLA Ops:
  6.5 0.7 all-gather.2.cloned.1.call-update
  7.3 2.5 broadcast_in_dim.6
  9.7 11.2 %all-to-all-start = ((bf16[32,4,16,512]{3,2,1,0:T(8,128)(2,1)}), bf16[32,4,16,512]{3,2,1,0:T(8,128)(2,1)S(1)}, u32[]{:S(2)}, u32[]{:S(2)}) async-start(bf16[32,4,16,512]{3,2,1,0:T(8,128)(2,1)} %broadcast_in_dim.6), calls=%async_computation | async-start | bytes 4194304 | tf_op jit(solution)/shard_map/all_to_all | solution.py:12
  21.0 4.1 %fusion.31 = (bf16[768,4]{0,1:T(4,128)(2,1)S(1)}, bf16[768,4,4]{0,2,1:T(4,128)(2,1)S(1)}) fusion(bf16[4,4,3328]{2,1,0:T(4,128)(2,1)S(1)} %dot_general.26, bf16[768,3328]{1,0:T(8,128)(2,1)} %param.7), kind=kOutput, calls=%fused_computation.31 | convolution fusion | flops 81810432 | bytes 5249024 | tf_op jit(solution)/shard_map/dot_general | solution.py:63
  25.1 0.6 copy.30
  25.7 27.7 %all-to-all-done = bf16[32,4,16,512]{3,2,1,0:T(8,128)(2,1)S(1)} async-done(((bf16[32,4,16,512]{3,2,1,0:T(8,128)(2,1)}), bf16[32,4,16,512]{3,2,1,0:T(8,128)(2,1)S(1)}, u32[]{:S(2)}, u32[]{:S(2)}) %all-to-all-start) | async-done | bytes 2097184 | tf_op jit(solution)/shard_map/all_to_all | solution.py:12
  53.4 0.6 broadcast_in_dim.7
  54.0 10.3 %all_to_all.20 = bf16[2,32,4,16,512]{4,3,2,1,0:T(8,128)(2,1)} all-to-all(bf16[2,32,4,16,512]{4,3,2,1,0:T(8,128)(2,1)S(1)} %broadcast_in_dim.7), channel_id=1, replica_groups=mesh['task'=2,'batch_0'=4,'batch_1'=2,'batch_2'=4,'batch_3'=2] {'batch_3'}, dimensions={0} | all-to-all | bytes 8388608 | tf_op jit(solution)/shard_map/all_to_all | solution.py:12
  64.3 1.1 broadcast_in_dim.8
  65.4 5.2 %all-to-all-start.2 = ((bf16[64,4,8,256]{3,2,1,0:T(8,128)(2,1)}), bf16[64,4,8,256]{3,2,1,0:T(8,128)(2,1)S(1)}, u32[]{:S(2)}, u32[]{:S(2)}) async-start(bf16[64,4,8,256]{3,2,1,0:T(8,128)(2,1)} %broadcast_in_dim.8), calls=%async_computation.2 | async-start | bytes 2097152 | tf_op jit(solution)/shard_map/all_to_all | solution.py:12
  70.7 2.7 %copy.26 = bf16[2,32,4,16,512]{4,3,2,0,1:T(8,128)(2,1)S(1)} copy(bf16[2,32,4,16,512]{4,3,2,1,0:T(8,128)(2,1)} %all_to_all.20) | data formatting | bytes 8388608 | tf_op jit(solution)/shard_map/all_to_all | solution.py:12
  73.4 2.5 copy.27
  75.9 104.4 %all-gather.2.cloned.1.call-done = bf16[4,3328,1024]{2,0,1:T(4,128)(2,1)} async-done(((bf16[4,52,1024]{2,0,1:T(4,128)(2,1)}), bf16[4,3328,1024]{2,0,1:T(4,128)(2,1)}) %all-gather.2.cloned.1.call-update) | async-done | bytes 27262992 | tf_op jit(solution)/shard_map/all_gather | solution.py:60
  180.3 39.0 %fusion.2 = bf16[4,768,512]{2,1,0:T(8,128)(2,1)} fusion(bf16[4,1024,512]{2,1,0:T(8,128)(2,1)} %bitcast.49, bf16[4,3328,1024]{2,0,1:T(4,128)(2,1)} %all-gather.2.cloned.1.call-done, bf16[768,3328]{1,0:T(8,128)(2,1)} %param.7), kind=kOutput, calls=%fused_computation.3 | convolution fusion | flops 24165482496 | bytes 39714816 | tf_op jit(solution)/shard_map/etr,erh->eth/dot_general | solution.py:72
  219.2 2.9 %maximum_convert_fusion.4 = bf16[4,768,256]{2,1,0:T(8,128)(2,1)S(1)} fusion(bf16[4,768,512]{2,1,0:T(8,128)(2,1)} %fusion.2, bf16[64,4,8,256]{3,2,1,0:T(8,128)(2,1)S(1)} %all-to-all-done.2), kind=kOutput, calls=%fused_computation.11 | convolution fusion | flops 811597824 | bytes 5767168 | tf_op jit(solution)/shard_map/etr,erh->eth/dot_general | solution.py:81
  222.1 1.4 convolution_convert_fusion
  223.6 0.8 concatenate.6
  224.4 3.1 %copy.32 = bf16[768,2,2,256]{0,2,3,1:T(2,128)(2,1)S(1)} copy(bf16[768,2,2,256]{3,2,1,0:T(2,128)(2,1)S(1)} %concatenate.6) | data formatting | bytes 3145728 | tf_op jit(solution)/shard_map/concatenate | solution.py:46
  227.5 2.0 maximum_bitcast_fusion
  229.5 21.6 %all_to_all.21 = bf16[2,768,2,257]{1,2,3,0:T(2,128)(2,1)S(1)} all-to-all(bf16[2,768,2,257]{1,2,3,0:T(2,128)(2,1)S(1)} %maximum_bitcast_fusion), channel_id=1, replica_groups=mesh['task'=2,'batch_0'=4,'batch_1'=2,'batch_2'=4,'batch_3'=2] {'task'}, dimensions={0} | all-to-all | bytes 3158016 | tf_op jit(solution)/shard_map/all_to_all | solution.py:40
  251.1 1.9 convert_reduce_fusion
  253.6 0.9 copy.41
  254.6 0.6 fusion.20
  255.1 0.6 copy.61
  (15 shorter events, 0.6 us)
Async XLA Ops:
  6.5 248.0 %copy-start = (bf16[2,256,128]{2,1,0:T(8,128)(2,1)S(1)}, bf16[2,256,128]{2,1,0:T(8,128)(2,1)}, u32[]{:S(2)}) copy-start(bf16[2,256,128]{2,1,0:T(8,128)(2,1)} %param.12) | copy-start | bytes 393220
  6.5 173.7 %all-gather.2.cloned.1.call-start = ((), (), s32[]{:S(2)}) async-start(), calls=%async_computation.4 | async-start | bytes 27688960 | tf_op jit(solution)/shard_map/all_gather | solution.py:60
  7.3 13.7 %copy-start.1 = (bf16[3328,4,4]{0,2,1:T(4,128)(2,1)S(1)}, bf16[3328,4,4]{0,2,1:T(4,128)(2,1)}, u32[]{:S(2)}) copy-start(bf16[3328,4,4]{0,2,1:T(4,128)(2,1)} %param.8) | copy-start | bytes 319492
  9.7 43.7 %all-to-all-start = ((bf16[32,4,16,512]{3,2,1,0:T(8,128)(2,1)}), bf16[32,4,16,512]{3,2,1,0:T(8,128)(2,1)S(1)}, u32[]{:S(2)}, u32[]{:S(2)}) async-start(bf16[32,4,16,512]{3,2,1,0:T(8,128)(2,1)} %broadcast_in_dim.6), calls=%async_computation | async-start | bytes 4194304 | tf_op jit(solution)/shard_map/all_to_all | solution.py:12
  54.0 10.3 %copy-start.2 = (bf16[4,8,256]{2,1,0:T(8,128)(2,1)S(1)}, bf16[4,8,256]{2,1,0:T(8,128)(2,1)}, u32[]{:S(2)}) copy-start(bf16[4,8,256]{2,1,0:T(8,128)(2,1)} %param.11) | copy-start | bytes 49156
  65.4 153.8 %all-to-all-start.2 = ((bf16[64,4,8,256]{3,2,1,0:T(8,128)(2,1)}), bf16[64,4,8,256]{3,2,1,0:T(8,128)(2,1)S(1)}, u32[]{:S(2)}, u32[]{:S(2)}) async-start(bf16[64,4,8,256]{3,2,1,0:T(8,128)(2,1)} %broadcast_in_dim.8), calls=%async_computation.2 | async-start | bytes 2097152 | tf_op jit(solution)/shard_map/all_to_all | solution.py:12
  253.0 1.5 copy-start.3
Sparse Core Ops, SparseCore 0:
  10.5 169.7 all-gather.1
where the time goes:
time: 263 us
  waiting for transfers between devices  133 us (51%)
  matrix products  47.9 us (18%)
  blocking collectives  31.9 us (12%)
  starting transfers between devices  16.4 us (6%)
  local copies, waits for them, and re-layouts  16.1 us (6%)
  between operations  13.6 us (5%)
  other arithmetic  3.92 us (1%)
    all_gather x1, waiting for transfers between devices, per_device(): gathered = lax.all_gather(w_first, BATCH, axis=1, tiled=True)  104 us
    dot_general x1, matrix products, per_device(): jnp.einsum('etr,erh->eth', columns, whole_of(w_second, (('batch_0', 'batc...  39 us
    all_to_all x2, waiting for transfers between devices, sent_to_all(): lax.all_to_all(jnp.broadcast_to(shard[None], (count, *shard.shape)), axis...  27.7 us
    all_to_all x1, blocking collectives, sent_and_summed(): parts = lax.all_to_all(in_blocks(shard, dim, count), axis, 0, 0, tiled=True)  21.6 us
    all_to_all x2, starting transfers between devices, sent_to_all(): lax.all_to_all(jnp.broadcast_to(shard[None], (count, *shard.shape)), axis...  16.4 us
    all_to_all x1, blocking collectives, sent_to_all(): lax.all_to_all(jnp.broadcast_to(shard[None], (count, *shard.shape)), axis...  10.3 us
  transfers between devices with their start and end apart: 3, of which 2 were waited for; matrix products, arithmetic and copies ran while one was open for 20% of the time, Pallas kernels for 0%

commit v1 on v0

v1 whole, which is shorter than its diff:
```python
import jax
import jax.numpy as jnp
from jax import lax
from jax.experimental import pallas as pl
from jax.experimental.pallas import tpu as pltpu
from jax.sharding import Mesh
from jax.sharding import PartitionSpec as P

AXES = ("task", "batch_0", "batch_1", "batch_2", "batch_3")
BATCH = AXES[1:]
MESH = pl.DeviceIdType.MESH
BF16 = jnp.bfloat16
F32 = jnp.float32

W1_ROWS, W2_ROWS, W3_ROWS = 52, 8, 4
QUAD = 4
BLOCK = W1_ROWS + W2_ROWS + W3_ROWS


def one_hot(rows, source):
    row = lax.broadcasted_iota(jnp.int32, (rows, QUAD * BLOCK), 0)
    column = lax.broadcasted_iota(jnp.int32, (rows, QUAD * BLOCK), 1)
    return jnp.where(source(row) == column, 1.0, 0.0).astype(BF16)


def picked(selector, values):
    return jnp.dot(selector, values, preferred_element_type=F32).astype(BF16)


def kernel(
    pooled_hbm, block_hbm, gate_hbm, hidden_ref, out_w_ref, out_ref,
    staged, w1, w23, pooled, gate, first, second, eo, numer, weights, send_sem, recv_sem, local_sem,
):
    t, y, zh, x, c = (lax.axis_index(a) for a in AXES)
    xp, xq = x // 2, lax.rem(x, 2)
    j = 2 * xq + c
    tq = jnp.where(zh == 1, t, 1 - t)
    experts = w1.shape[0]
    tokens = pooled.shape[0]

    def at(pos, k):
        return lax.rem(pos + (k + 4), 4)

    core_peer = (t, y, zh, x, 1 - c)
    z_peer = (1 - t, y, 1 - zh, x, c)
    task_peer = (1 - t, y, zh, x, c)
    x_dev = lambda k: (t, y, zh, at(x, k), c)
    y_dev = lambda k: (t, at(y, k), zh, x, c)

    def quad_dev(d):
        dx, dc = d // 2, d % 2
        return (tq, y, zh, 2 * xp + (1 - xq if dx else xq), 1 - c if dc else c)

    used = [0]
    sent = []

    def slot():
        used[0] += 1
        return used[0] - 1

    def push(i, src, dst, device):
        copy = pltpu.make_async_remote_copy(
            src_ref=src, dst_ref=dst, send_sem=send_sem.at[i], recv_sem=recv_sem.at[i],
            device_id=device, device_id_type=MESH,
        )
        copy.start()
        sent.append(copy)

    def arrived(i, dst):
        pltpu.make_async_remote_copy(
            src_ref=dst, dst_ref=dst, send_sem=send_sem.at[i], recv_sem=recv_sem.at[i],
            device_id=core_peer, device_id_type=MESH,
        ).wait_recv()

    half = tokens // 2
    loads = [
        pltpu.make_async_copy(pooled_hbm.at[pl.ds(k * half, half)], pooled.at[pl.ds(k * half, half)], local_sem.at[k])
        for k in range(2)
    ]
    loads.append(pltpu.make_async_copy(gate_hbm.at[t], gate.at[0], local_sem.at[2]))
    own_block = pltpu.make_async_copy(block_hbm.at[j], staged.at[j], local_sem.at[3])
    for load in loads:
        load.start()

    @pl.when(zh == 1)
    def _():
        own_block.start()

    barrier = pltpu.get_barrier_semaphore()
    peers = [x_dev(1), x_dev(-1), y_dev(1), y_dev(-1), z_peer, core_peer, task_peer] + [quad_dev(d) for d in range(1, QUAD)]
    for device in peers:
        pl.semaphore_signal(barrier, inc=1, device_id=device, device_id_type=MESH)
    pl.semaphore_wait(barrier, len(peers))

    quad_slots = [slot() for _ in range(QUAD)]
    for d in range(1, QUAD):
        to = 2 * ((1 - xq) if d // 2 else xq) + ((1 - c) if d % 2 else c)
        push(quad_slots[d], block_hbm.at[to], staged.at[j], quad_dev(d))
    own_far = pltpu.make_async_remote_copy(
        src_ref=block_hbm.at[j], dst_ref=staged.at[j], send_sem=send_sem.at[quad_slots[0]],
        recv_sem=recv_sem.at[quad_slots[0]], device_id=task_peer, device_id_type=MESH,
    )

    @pl.when(zh == 0)
    def _():
        own_far.start()

    gate_slot = slot()
    push(gate_slot, gate_hbm.at[1 - t], gate.at[1], task_peer)

    for d in range(1, QUAD):
        arrived(quad_slots[d], staged.at[2 * ((1 - xq) if d // 2 else xq) + ((1 - c) if d % 2 else c)])

    @pl.when(zh == 1)
    def _():
        own_block.wait()

    @pl.when(zh == 0)
    def _():
        own_far.wait()

    def w1_source(r):
        return r + (BLOCK - W1_ROWS) * (
            (r >= W1_ROWS).astype(jnp.int32) + (r >= 2 * W1_ROWS).astype(jnp.int32) + (r >= 3 * W1_ROWS).astype(jnp.int32)
        )

    def half_source(r, unit, side, base):
        member, within = r // (2 * unit), lax.rem(r, 2 * unit)
        return jnp.where(within // unit == side, BLOCK * member + base + lax.rem(within, unit), -1)

    pick1 = one_hot(QUAD * W1_ROWS, w1_source)
    pick2 = [one_hot(QUAD * 16, lambda r, s=s: half_source(r, W2_ROWS, s, W1_ROWS)) for s in range(2)]
    pick3 = [
        one_hot(16, lambda r, s=s: jnp.where(
            half_source(r, W3_ROWS, s, W1_ROWS + W2_ROWS) >= 0,
            half_source(r, W3_ROWS, s, W1_ROWS + W2_ROWS) + 2 * BLOCK * xq, -1))
        for s in range(2)
    ]
    col0 = pl.multiple_of(512 * c, 128)

    def w1_cols(h, xq_):
        return pl.ds(pl.multiple_of(512 * c + 256 * h + 128 * xq_, 128), 128)

    for e in range(experts):
        rows = staged[:, e].reshape(QUAD * BLOCK, 256)
        w1_part = picked(pick1, rows)
        w1[e, y, zh, xp, :, w1_cols(0, xq)] = w1_part[:, :128]
        w1[e, y, zh, xp, :, w1_cols(1, xq)] = w1_part[:, 128:]
        w23[e % 2, e // 2, y, zh, xp, xq, c, 0:64] = picked(
            jnp.concatenate(pick2, axis=1), jnp.concatenate([rows[:, :128], rows[:, 128:]], axis=0)
        )
        w23[e % 2, e // 2, y, zh, xp, xq, c, 64:80] = picked(
            jnp.concatenate(pick3, axis=1), jnp.concatenate([rows[:, :128], rows[:, 128:]], axis=0)
        )

    def plane(o):
        return zh if o == 0 else 1 - zh

    def a1(k, o):
        x_ = at(x, k)
        return w1.at[:, y, plane(o), x_ // 2, :, w1_cols(0, lax.rem(x_, 2))]

    def b1(k, o):
        return w1.at[:, at(y, k), plane(o), xp, :, w1_cols(1, xq)]

    def c1x(k, o):
        x_ = at(x, k)
        return w23.at[0, :, y, plane(o), x_ // 2, lax.rem(x_, 2), c]

    def c1y(k, o):
        return w23.at[1, :, at(y, k), plane(o), xp, xq, c]

    def a2(e, k, o, core):
        return w1.at[e, at(y, k), plane(o), :, :, pl.ds(pl.multiple_of(512 * core, 128), 256)]

    def b2(e, k, o, core):
        x_ = at(x, k)
        cols = pl.ds(pl.multiple_of(512 * core + 256 + 128 * lax.rem(x_, 2), 128), 128)
        return w1.at[e, :, plane(o), x_ // 2, :, cols]

    def c2(e, k, o, core):
        if e % 2 == 0:
            return w23.at[0, e // 2, at(y, k), plane(o), :, :, core]
        x_ = at(x, k)
        return w23.at[1, e // 2, :, plane(o), x_ // 2, lax.rem(x_, 2), core]

    class Ring:
        def __init__(self, device, part):
            self.device, self.part = device, part
            self.slots = {(o, k): slot() for o in range(2) for k in (1, -1, 2)}

        def near(self, o):
            for k in (1, -1):
                push(self.slots[o, k], self.part(0, o), self.part(0, o), self.device(k))

        def near_arrived(self, o):
            for k in (1, -1):
                arrived(self.slots[o, k], self.part(-k, o))

        def far(self, o):
            k = 1 if o == 0 else -1
            push(self.slots[o, 2], self.part(-k, o), self.part(-k, o), self.device(k))

        def far_arrived(self, o):
            arrived(self.slots[o, 2], self.part(2, o))

    one = [Ring(x_dev, a1), Ring(y_dev, b1), Ring(x_dev, c1x), Ring(y_dev, c1y)]
    two, shared = [], []
    for e in range(experts):
        parts = [
            (y_dev, lambda k, o, core=c, e=e: a2(e, k, o, core)),
            (x_dev, lambda k, o, core=c, e=e: b2(e, k, o, core)),
            (y_dev if e % 2 == 0 else x_dev, lambda k, o, core=c, e=e: c2(e, k, o, core)),
        ]
        two.append([Ring(device, part) for device, part in parts])
        shared.append([(part, {(k, o): slot() for k in (0, 1, -1, 2) for o in range(2)}) for _, part in parts])

    def share(e, which):
        for part, slots in shared[e]:
            for k in which:
                for o in range(2):
                    push(slots[k, o], part(k, o), part(k, o), core_peer)

    def share_arrived(e):
        for part, slots in shared[e]:
            for (k, o), i in slots.items():
                arrived(i, part(k, o, 1 - c))

    def each(rings, step, o):
        for ring in rings:
            getattr(ring, step)(o)

    z_slots = [slot() for _ in one]
    for ring, i in zip(one, z_slots):
        push(i, ring.part(0, 0), ring.part(0, 0), z_peer)
    each(one, "near", 0)

    for load in loads:
        load.wait()
    arrived(gate_slot, gate.at[1])
    own_gate = jnp.where(zh == 1, 0, 1)
    for o in range(2):
        g = gate[own_gate if o == 0 else 1 - own_gate]
        logits = lax.dot_general(pooled[...], g, (((1,), (1,)), ((), ())), preferred_element_type=F32)
        weights[o] = jnp.exp(logits)
    numer[...] = jnp.zeros_like(numer)

    each(one, "near_arrived", 0)
    each(one, "far", 0)
    each(one, "far_arrived", 0)
    each(two[0], "near", 0)
    for ring, i in zip(one, z_slots):
        arrived(i, ring.part(0, 1))
    each(one, "near", 1)
    each(one, "near_arrived", 1)
    each(one, "far", 1)
    each(one, "far_arrived", 1)
    each(two[0], "near", 1)
    for o in range(2):
        each(two[1], "near", o)

    eo_slots = [slot() for _ in range(experts)]
    assert used[0] <= send_sem.shape[0], used[0]

    def near_done(e):
        for o in range(2):
            each(two[e], "near_arrived", o)
            each(two[e], "far", o)
        share(e, (0, 1, -1))
        if e + 2 < experts:
            for o in range(2):
                each(two[e + 2], "near", o)

    def far_done(e):
        for o in range(2):
            each(two[e], "far_arrived", o)
        share(e, (2,))

    def add_up(o, e):
        values = eo[o, e].astype(F32)
        for k in range(2):
            numer[k] += weights[o, :, 2 * e + k : 2 * e + k + 1] * values

    def compute(e):
        @pl.loop(0, 4)
        def _(n):
            cols = pl.ds(pl.multiple_of(n * 256, 256), 256)
            w = w1[e, :, :, :, :, cols].reshape(16 * 208, 256)
            summed = jnp.dot(pooled[...], w, preferred_element_type=F32)
            first[:, cols] = jnp.maximum(summed, 0.0).astype(BF16)

        @pl.loop(0, 2)
        def _(n):
            cols = pl.ds(pl.multiple_of(n * 256, 256), 256)
            w = jnp.concatenate(
                [w23[e % 2, e // 2, :, :, :, q, n, 0:64].reshape(16 * 64, 128) for q in range(2)], axis=1
            )
            summed = jnp.dot(first[...], w, preferred_element_type=F32)
            second[:, cols] = jnp.maximum(summed, 0.0).astype(BF16)

        w = jnp.concatenate(
            [w23[e % 2, e // 2, :, :, :, :, n, 64:80].reshape(32 * 16, 128) for n in range(2)], axis=1
        )
        summed = jnp.dot(second[...], w, preferred_element_type=F32)
        eo[0, e] = jnp.maximum(summed, 0.0).astype(BF16)
        push(eo_slots[e], eo.at[0, e], eo.at[1, e], task_peer)
        add_up(0, e)

    near_done(0)
    near_done(1)
    far_done(0)
    for e in range(experts):
        share_arrived(e)
        compute(e)
        if e + 2 < experts:
            near_done(e + 2)
        if e + 1 < experts:
            far_done(e + 1)
    for e in range(experts):
        arrived(eo_slots[e], eo.at[1, e])
        add_up(1, e)

    for k in range(2):
        total = sum(weights[o, :, 2 * e + k : 2 * e + k + 1] for o in range(2) for e in range(experts))
        mix = (numer[k] / total).astype(BF16)
        tower = jnp.maximum(jnp.dot(mix, hidden_ref[k], preferred_element_type=F32), 0.0).astype(BF16)
        out_ref[:, k : k + 1] = jnp.sum(tower.astype(F32) * out_w_ref[k : k + 1, :].astype(F32), axis=1, keepdims=True)

    for copy in sent:
        copy.wait_send()


def per_device(pooled, gate_weight, w_first, w_second, w_third, tower_hidden, tower_out):
    tokens, width = pooled.shape
    experts = w_first.shape[0]
    one = w_first.reshape(experts, 52, 2, 2, 2, 128).transpose(4, 2, 0, 1, 3, 5).reshape(4, experts, 52, 256)
    two = w_second.reshape(experts, 2, 8, 2, 2, 128).transpose(4, 3, 0, 2, 1, 5).reshape(4, experts, 8, 256)
    three = w_third.reshape(experts, 2, 4, 2, 128).transpose(3, 0, 2, 1, 4).reshape(1, 2, experts, 4, 256)
    three = jnp.broadcast_to(three, (2, 2, experts, 4, 256)).reshape(4, experts, 4, 256)
    block = jnp.concatenate([one, two, three], axis=2)
    gate = gate_weight.reshape(width, experts, 2, 2).transpose(2, 1, 3, 0).reshape(2, 2 * experts, width)
    any_, vmem = pl.BlockSpec(memory_space=pl.ANY), pl.BlockSpec(memory_space=pltpu.VMEM)
    slots = 300
    return pl.pallas_call(
        kernel,
        out_shape=jax.ShapeDtypeStruct((tokens, 2), F32),
        in_specs=[any_, any_, any_, vmem, vmem],
        out_specs=vmem,
        scratch_shapes=[
            pltpu.VMEM((QUAD, experts, BLOCK, 256), BF16),
            pltpu.VMEM((experts, 4, 2, 2, 208, 1024), BF16),
            pltpu.VMEM((2, 2, 4, 2, 2, 2, 2, 80, 128), BF16),
            pltpu.VMEM((tokens, width), BF16),
            pltpu.VMEM((2, 2 * experts, width), BF16),
            pltpu.VMEM((tokens, 1024), BF16),
            pltpu.VMEM((tokens, 512), BF16),
            pltpu.VMEM((2, experts, tokens, 256), BF16),
            pltpu.VMEM((2, tokens, 256), F32),
            pltpu.VMEM((2, tokens, 2 * experts), F32),
            pltpu.SemaphoreType.DMA((slots,)),
            pltpu.SemaphoreType.DMA((slots,)),
            pltpu.SemaphoreType.DMA((4,)),
        ],
        compiler_params=pltpu.CompilerParams(
            collective_id=0, has_side_effects=True, vmem_limit_bytes=67_000_000
        ),
    )(pooled, block, gate, tower_hidden, tower_out)


def solution(mesh):
    torus = Mesh(mesh.devices.reshape(mesh.shape["task"], 4, 2, 4, 2), AXES)
    return jax.shard_map(
        per_device,
        mesh=torus,
        in_specs=(
            P(BATCH, None),
            P(None, "task", None),
            P("task", BATCH, None),
            P("task", BATCH, None),
            P("task", BATCH, None),
            P("task", None, None),
            P("task", None),
        ),
        out_specs=P(BATCH, "task"),
        check_vma=False,
    )
```

time: 263 us -> 159 us (0.60)
  Pallas kernels: 0 us -> 151 us
  waiting for transfers between devices: 133 us -> 0 us
  matrix products: 47.9 us -> 0 us
  blocking collectives: 31.9 us -> 0 us
  starting transfers between devices: 16.4 us -> 0 us
  between operations: 13.6 us -> 0.06 us
  local copies, waits for them, and re-layouts: 16.1 us -> 6.77 us
  other arithmetic: 3.92 us -> 0.88 us
    pallas_call x0 -> x1, Pallas kernels: none -> 151 us  [per_device(): pl.pallas_call(kernel, out_shape=jax.ShapeDtypeStruct((tokens, 2), F32),...]
    all_gather x1 -> x0, waiting for transfers between devices: 104 us -> none  [per_device(): gathered = lax.all_gather(w_first, BATCH, axis=1, tiled=True)]
    dot_general x5 -> x0, matrix products: 47.9 us -> none  [the longest x1 39 us: per_device(): jnp.einsum('etr,erh->eth', columns, whole_of(w_second, (('batch_0', 'batc...]
    all_to_all x2 -> x0, blocking collectives: 31.9 us -> none  [the longest x1 21.6 us: sent_and_summed(): parts = lax.all_to_all(in_blocks(shard, dim, count), axis, 0, 0, tiled=True)]
    all_to_all x2 -> x0, waiting for transfers between devices: 27.7 us -> none  [sent_to_all(): lax.all_to_all(jnp.broadcast_to(shard[None], (count, *shard.shape)), axis...]
    all_to_all x2 -> x0, starting transfers between devices: 16.4 us -> none  [sent_to_all(): lax.all_to_all(jnp.broadcast_to(shard[None], (count, *shard.shape)), axis...]
    reshape x1 -> x10, local copies, waits for them, and re-layouts: 0.03 us -> 5.02 us  [the longest x4 1.73 us: per_device(): w_first.reshape(experts, 52, 2, 2, 2, 128).transpose(4, 2, 0, 1, 3, 5)]
    broadcast_in_dim x3 -> x1, local copies, waits for them, and re-layouts: 4.19 us -> 0.01 us  [per_device(): jnp.broadcast_to(three, (2, 2, experts, 4, 256)).reshape(4, experts, 4, 256)]
  transfers between devices with their start and end apart: 3 -> 0, of which waited for: 2 -> 0; matrix products, arithmetic and copies ran while one was open for 20% -> 0% of each run, Pallas kernels for 0% -> 0%
where the time goes in v1:
time: 159 us; the launch traced here: 158 us
  Pallas kernels  151 us (95%)
  local copies, waits for them, and re-layouts  6.77 us (4%)
    pallas_call x1, Pallas kernels, per_device(): pl.pallas_call(kernel, out_shape=jax.ShapeDtypeStruct((tokens, 2), F32),...  151 us

profile of v1, /device:TPU:1, one launch (start us, length us, event | category | flops | bytes accessed | tf_op | source)
XLA Modules:
  0.0 158.2 jit_solution(2051223462179081698)
XLA Ops:
  0.0 1.2 reshape.26
  1.2 0.2 copy.21
  1.4 0.3 reshape.27
  1.7 0.1 copy.15
  1.8 0.9 copy.13
  2.6 0.7 reshape.30
  3.4 0.9 pad_maximum_fusion.block_hbm
  4.2 0.9 reshape.32
  5.2 0.1 copy.22
  5.3 0.7 reshape.33.gate_hbm
  6.0 150.5 %shard_map.73 = f32[768,2]{1,0:T(8,128)} custom-call(bf16[768,3328]{1,0:T(8,128)(2,1)} %pooled_hbm.1, bf16[4,4,64,256]{3,2,1,0:T(8,128)(2,1)} %pad_maximum_fusion.block_hbm, bf16[2,8,3328]{2,1,0:T(8,128)(2,1)} %reshape.33.gate_hbm, bf16[2,256,128]{2,1,0:T(8,128)(2,1)} %hidden_ref.1, bf16[2,128]{1,0:T(2,128)(2,1)} %out_w_ref.1), custom_call_target="tpu_custom_call" | custom-call | tf_op jit(solution)/shard_map/pallas_call | solution.py:344
  156.5 1.7 %copy.17 = f32[768,2]{0,1:T(2,128)} copy(f32[768,2]{1,0:T(8,128)} %shard_map.73) | data formatting | bytes 12288 | tf_op jit(solution)/shard_map/pallas_call | solution.py:344
  (2 shorter events, 0.0 us)

commit v2 on v1

--- a/solution.py
+++ b/solution.py
@@ -92,32 +92,29 @@
         pl.semaphore_signal(barrier, inc=1, device_id=device, device_id_type=MESH)
     pl.semaphore_wait(barrier, len(peers))
 
-    quad_slots = [slot() for _ in range(QUAD)]
-    for d in range(1, QUAD):
-        to = 2 * ((1 - xq) if d // 2 else xq) + ((1 - c) if d % 2 else c)
-        push(quad_slots[d], block_hbm.at[to], staged.at[j], quad_dev(d))
-    own_far = pltpu.make_async_remote_copy(
-        src_ref=block_hbm.at[j], dst_ref=staged.at[j], send_sem=send_sem.at[quad_slots[0]],
-        recv_sem=recv_sem.at[quad_slots[0]], device_id=task_peer, device_id_type=MESH,
-    )
-
-    @pl.when(zh == 0)
-    def _():
-        own_far.start()
+    def member(d):
+        return 2 * ((1 - xq) if d // 2 else xq) + ((1 - c) if d % 2 else c)
+
+    quad_slots = [[slot() for _ in range(QUAD)] for _ in range(experts)]
+    own_far = []
+    for e in range(experts):
+        for d in range(1, QUAD):
+            push(quad_slots[e][d], block_hbm.at[member(d), e], staged.at[j, e], quad_dev(d))
+        own_far.append(pltpu.make_async_remote_copy(
+            src_ref=block_hbm.at[j, e], dst_ref=staged.at[j, e], send_sem=send_sem.at[quad_slots[e][0]],
+            recv_sem=recv_sem.at[quad_slots[e][0]], device_id=task_peer, device_id_type=MESH,
+        ))
+
+        @pl.when(zh == 0)
+        def _(e=e):
+            own_far[e].start()
 
     gate_slot = slot()
     push(gate_slot, gate_hbm.at[1 - t], gate.at[1], task_peer)
-
-    for d in range(1, QUAD):
-        arrived(quad_slots[d], staged.at[2 * ((1 - xq) if d // 2 else xq) + ((1 - c) if d % 2 else c)])
 
     @pl.when(zh == 1)
     def _():
         own_block.wait()
-
-    @pl.when(zh == 0)
-    def _():
-        own_far.wait()
 
     def w1_source(r):
         return r + (BLOCK - W1_ROWS) * (
@@ -141,7 +138,14 @@
     def w1_cols(h, xq_):
         return pl.ds(pl.multiple_of(512 * c + 256 * h + 128 * xq_, 128), 128)
 
-    for e in range(experts):
+    def pack(e):
+        for d in range(1, QUAD):
+            arrived(quad_slots[e][d], staged.at[member(d), e])
+
+        @pl.when(zh == 0)
+        def _():
+            own_far[e].wait()
+
         rows = staged[:, e].reshape(QUAD * BLOCK, 256)
         w1_part = picked(pick1, rows)
         w1[e, y, zh, xp, :, w1_cols(0, xq)] = w1_part[:, :128]
@@ -156,19 +160,18 @@
     def plane(o):
         return zh if o == 0 else 1 - zh
 
-    def a1(k, o):
+    def a1(e, k):
         x_ = at(x, k)
-        return w1.at[:, y, plane(o), x_ // 2, :, w1_cols(0, lax.rem(x_, 2))]
-
-    def b1(k, o):
-        return w1.at[:, at(y, k), plane(o), xp, :, w1_cols(1, xq)]
-
-    def c1x(k, o):
-        x_ = at(x, k)
-        return w23.at[0, :, y, plane(o), x_ // 2, lax.rem(x_, 2), c]
-
-    def c1y(k, o):
-        return w23.at[1, :, at(y, k), plane(o), xp, xq, c]
+        return w1.at[e, y, zh, x_ // 2, :, w1_cols(0, lax.rem(x_, 2))]
+
+    def b1(e, k):
+        return w1.at[e, at(y, k), zh, xp, :, w1_cols(1, xq)]
+
+    def c1(e, k):
+        if e % 2 == 0:
+            x_ = at(x, k)
+            return w23.at[0, e // 2, y, zh, x_ // 2, lax.rem(x_, 2), c]
+        return w23.at[1, e // 2, at(y, k), zh, xp, xq, c]
 
     def a2(e, k, o, core):
         return w1.at[e, at(y, k), plane(o), :, :, pl.ds(pl.multiple_of(512 * core, 128), 256)]
@@ -185,109 +188,115 @@
         return w23.at[1, e // 2, :, plane(o), x_ // 2, lax.rem(x_, 2), core]
 
     class Ring:
-        def __init__(self, device, part):
-            self.device, self.part = device, part
-            self.slots = {(o, k): slot() for o in range(2) for k in (1, -1, 2)}
-
-        def near(self, o):
+        def __init__(self, device, part, way):
+            self.device, self.part, self.way = device, part, way
+            self.slots = {k: slot() for k in (1, -1, 2)}
+
+        def near(self):
             for k in (1, -1):
-                push(self.slots[o, k], self.part(0, o), self.part(0, o), self.device(k))
-
-        def near_arrived(self, o):
+                push(self.slots[k], self.part(0), self.part(0), self.device(k))
+
+        def near_arrived(self):
             for k in (1, -1):
-                arrived(self.slots[o, k], self.part(-k, o))
-
-        def far(self, o):
-            k = 1 if o == 0 else -1
-            push(self.slots[o, 2], self.part(-k, o), self.part(-k, o), self.device(k))
-
-        def far_arrived(self, o):
-            arrived(self.slots[o, 2], self.part(2, o))
-
-    one = [Ring(x_dev, a1), Ring(y_dev, b1), Ring(x_dev, c1x), Ring(y_dev, c1y)]
-    two, shared = [], []
+                arrived(self.slots[k], self.part(-k))
+
+        def far(self):
+            self.near_arrived()
+            k = self.way
+            push(self.slots[2], self.part(-k), self.part(-k), self.device(k))
+
+        def far_arrived(self):
+            arrived(self.slots[2], self.part(2))
+
+    one, two, z_slots, shared = [], [], [], []
     for e in range(experts):
+        third = y_dev if e % 2 == 0 else x_dev
+        first_third = x_dev if e % 2 == 0 else y_dev
         parts = [
-            (y_dev, lambda k, o, core=c, e=e: a2(e, k, o, core)),
-            (x_dev, lambda k, o, core=c, e=e: b2(e, k, o, core)),
-            (y_dev if e % 2 == 0 else x_dev, lambda k, o, core=c, e=e: c2(e, k, o, core)),
+            (x_dev, lambda k, e=e: a1(e, k), y_dev, lambda k, o, core=c, e=e: a2(e, k, o, core)),
+            (y_dev, lambda k, e=e: b1(e, k), x_dev, lambda k, o, core=c, e=e: b2(e, k, o, core)),
+            (first_third, lambda k, e=e: c1(e, k), third, lambda k, o, core=c, e=e: c2(e, k, o, core)),
         ]
-        two.append([Ring(device, part) for device, part in parts])
-        shared.append([(part, {(k, o): slot() for k in (0, 1, -1, 2) for o in range(2)}) for _, part in parts])
-
-    def share(e, which):
+        one.append([Ring(d1, p1, 1 if (e + i) % 2 == 0 else -1) for i, (d1, p1, _, _) in enumerate(parts)])
+        two.append([
+            [Ring(d2, lambda k, p2=p2, o=o: p2(k, o), 1 if o == 0 else -1) for _, _, d2, p2 in parts] for o in range(2)
+        ])
+        z_slots.append([slot() for _ in parts])
+        shared.append([(p2, {(k, o): slot() for k in (0, 1, -1, 2) for o in range(2)}) for _, _, _, p2 in parts])
+
+    def share(e, o, which):
         for part, slots in shared[e]:
             for k in which:
-                for o in range(2):
-                    push(slots[k, o], part(k, o), part(k, o), core_peer)
+                push(slots[k, o], part(k, o), part(k, o), core_peer)
 
     def share_arrived(e):
         for part, slots in shared[e]:
             for (k, o), i in slots.items():
                 arrived(i, part(k, o, 1 - c))
 
-    def each(rings, step, o):
+    def each(rings, step):
         for ring in rings:
-            getattr(ring, step)(o)
-
-    z_slots = [slot() for _ in one]
-    for ring, i in zip(one, z_slots):
-        push(i, ring.part(0, 0), ring.part(0, 0), z_peer)
-    each(one, "near", 0)
-
-    for load in loads:
-        load.wait()
-    arrived(gate_slot, gate.at[1])
-    own_gate = jnp.where(zh == 1, 0, 1)
-    for o in range(2):
-        g = gate[own_gate if o == 0 else 1 - own_gate]
-        logits = lax.dot_general(pooled[...], g, (((1,), (1,)), ((), ())), preferred_element_type=F32)
-        weights[o] = jnp.exp(logits)
-    numer[...] = jnp.zeros_like(numer)
-
-    each(one, "near_arrived", 0)
-    each(one, "far", 0)
-    each(one, "far_arrived", 0)
-    each(two[0], "near", 0)
-    for ring, i in zip(one, z_slots):
-        arrived(i, ring.part(0, 1))
-    each(one, "near", 1)
-    each(one, "near_arrived", 1)
-    each(one, "far", 1)
-    each(one, "far_arrived", 1)
-    each(two[0], "near", 1)
-    for o in range(2):
-        each(two[1], "near", o)
+            getattr(ring, step)()
+
+    def first_round(e):
+        pack(e)
+        each(one[e], "near")
+
+    def first_far(e):
+        each(one[e], "far")
+
+    def first_done(e):
+        each(one[e], "far_arrived")
+        for (part, _), i in zip(shared[e], z_slots[e]):
+            push(i, part(0, 0), part(0, 0), z_peer)
+
+    def near(e, o):
+        each(two[e][o], "near")
+
+    def z_done(e):
+        for (part, _), i in zip(shared[e], z_slots[e]):
+            arrived(i, part(0, 1))
+        near(e, 1)
+
+    def far(e, o):
+        each(two[e][o], "far")
+        share(e, o, (0, 1, -1))
+
+    def far_done(e):
+        for o in range(2):
+            each(two[e][o], "far_arrived")
+            share(e, o, (2,))
+
+    def gates():
+        for load in loads:
+            load.wait()
+        arrived(gate_slot, gate.at[1])
+        own_gate = jnp.where(zh == 1, 0, 1)
+        for o in range(2):
+            g = gate[own_gate if o == 0 else 1 - own_gate]
+            logits = lax.dot_general(pooled[...], g, (((1,), (1,)), ((), ())), preferred_element_type=F32)
+            weights[o] = jnp.exp(logits)
+        numer[...] = jnp.zeros_like(numer)
 
     eo_slots = [slot() for _ in range(experts)]
     assert used[0] <= send_sem.shape[0], used[0]
-
-    def near_done(e):
-        for o in range(2):
-            each(two[e], "near_arrived", o)
-            each(two[e], "far", o)
-        share(e, (0, 1, -1))
-        if e + 2 < experts:
-            for o in range(2):
-                each(two[e + 2], "near", o)
-
-    def far_done(e):
-        for o in range(2):
-            each(two[e], "far_arrived", o)
-        share(e, (2,))
 
     def add_up(o, e):
         values = eo[o, e].astype(F32)
         for k in range(2):
             numer[k] += weights[o, :, 2 * e + k : 2 * e + k + 1] * values
 
-    def compute(e):
-        @pl.loop(0, 4)
-        def _(n):
-            cols = pl.ds(pl.multiple_of(n * 256, 256), 256)
-            w = w1[e, :, :, :, :, cols].reshape(16 * 208, 256)
-            summed = jnp.dot(pooled[...], w, preferred_element_type=F32)
-            first[:, cols] = jnp.maximum(summed, 0.0).astype(BF16)
+    def compute(e, between=None):
+        for start in range(0, 4, 2):
+            @pl.loop(start, start + 2)
+            def _(n):
+                cols = pl.ds(pl.multiple_of(n * 256, 256), 256)
+                w = w1[e, :, :, :, :, cols].reshape(16 * 208, 256)
+                summed = jnp.dot(pooled[...], w, preferred_element_type=F32)
+                first[:, cols] = jnp.maximum(summed, 0.0).astype(BF16)
+
+            if start == 0 and between is not None:
+                between()
 
         @pl.loop(0, 2)
         def _(n):
@@ -306,16 +315,44 @@
         push(eo_slots[e], eo.at[0, e], eo.at[1, e], task_peer)
         add_up(0, e)
 
-    near_done(0)
-    near_done(1)
+    first_round(0)
+    first_round(1)
+    first_far(0)
+    first_round(2)
+    first_done(0)
+    near(0, 0)
+    first_far(1)
+    first_round(3)
+    first_done(1)
+    near(1, 0)
+    first_far(2)
+    gates()
+    z_done(0)
+    far(0, 0)
+    first_done(2)
+    near(2, 0)
+    first_far(3)
+    far(0, 1)
+    first_done(3)
+    z_done(1)
+    far(1, 0)
     far_done(0)
-    for e in range(experts):
-        share_arrived(e)
-        compute(e)
-        if e + 2 < experts:
-            near_done(e + 2)
-        if e + 1 < experts:
-            far_done(e + 1)
+    near(3, 0)
+    share_arrived(0)
+    compute(0, lambda: far(1, 1))
+    z_done(2)
+    far(2, 0)
+    far_done(1)
+    share_arrived(1)
+    compute(1, lambda: far(2, 1))
+    z_done(3)
+    far(3, 0)
+    far_done(2)
+    share_arrived(2)
+    compute(2, lambda: far(3, 1))
+    far_done(3)
+    share_arrived(3)
+    compute(3)
     for e in range(experts):
         arrived(eo_slots[e], eo.at[1, e])
         add_up(1, e)

time: 159 us -> 142 us (0.89)
  Pallas kernels: 151 us -> 134 us
    pallas_call x1, Pallas kernels: 151 us -> 134 us  [per_device(): pl.pallas_call(kernel, out_shape=jax.ShapeDtypeStruct((tokens, 2), F32),...]
where the time goes in v2:
time: 142 us
  Pallas kernels  134 us (94%)
  local copies, waits for them, and re-layouts  6.77 us (5%)
    pallas_call x1, Pallas kernels, per_device(): pl.pallas_call(kernel, out_shape=jax.ShapeDtypeStruct((tokens, 2), F32),...  134 us

profile of v2, /device:TPU:1, one launch (start us, length us, event | category | flops | bytes accessed | tf_op | source)
XLA Modules:
  0.0 141.9 jit_solution(6223764793126885725)
XLA Ops:
  0.0 1.2 reshape.26
  1.2 0.2 copy.21
  1.4 0.3 reshape.27
  1.7 0.1 copy.15
  1.8 0.9 copy.13
  2.6 0.7 reshape.30
  3.4 0.9 pad_maximum_fusion.block_hbm
  4.2 0.9 reshape.32
  5.2 0.1 copy.22
  5.3 0.7 reshape.33.gate_hbm
  6.0 134.2 %shard_map.73 = f32[768,2]{1,0:T(8,128)} custom-call(bf16[768,3328]{1,0:T(8,128)(2,1)} %pooled_hbm.1, bf16[4,4,64,256]{3,2,1,0:T(8,128)(2,1)} %pad_maximum_fusion.block_hbm, bf16[2,8,3328]{2,1,0:T(8,128)(2,1)} %reshape.33.gate_hbm, bf16[2,256,128]{2,1,0:T(8,128)(2,1)} %hidden_ref.1, bf16[2,128]{1,0:T(2,128)(2,1)} %out_w_ref.1), custom_call_target="tpu_custom_call" | custom-call | tf_op jit(solution)/shard_map/pallas_call | solution.py:381
  140.2 1.7 %copy.17 = f32[768,2]{0,1:T(2,128)} copy(f32[768,2]{1,0:T(8,128)} %shard_map.73) | data formatting | bytes 12288 | tf_op jit(solution)/shard_map/pallas_call | solution.py:381
  (2 shorter events, 0.0 us)

commit v3 on v2

--- a/solution.py
+++ b/solution.py
@@ -1,3 +1,5 @@
+import functools
+
 import jax
 import jax.numpy as jnp
 from jax import lax
@@ -96,21 +98,25 @@
         return 2 * ((1 - xq) if d // 2 else xq) + ((1 - c) if d % 2 else c)
 
     quad_slots = [[slot() for _ in range(QUAD)] for _ in range(experts)]
-    own_far = []
-    for e in range(experts):
+    own_far = [
+        pltpu.make_async_remote_copy(
+            src_ref=block_hbm.at[j, e], dst_ref=staged.at[j, e], send_sem=send_sem.at[quad_slots[e][0]],
+            recv_sem=recv_sem.at[quad_slots[e][0]], device_id=task_peer, device_id_type=MESH,
+        )
+        for e in range(experts)
+    ]
+
+    def quad(e):
         for d in range(1, QUAD):
             push(quad_slots[e][d], block_hbm.at[member(d), e], staged.at[j, e], quad_dev(d))
-        own_far.append(pltpu.make_async_remote_copy(
-            src_ref=block_hbm.at[j, e], dst_ref=staged.at[j, e], send_sem=send_sem.at[quad_slots[e][0]],
-            recv_sem=recv_sem.at[quad_slots[e][0]], device_id=task_peer, device_id_type=MESH,
-        ))
 
         @pl.when(zh == 0)
-        def _(e=e):
+        def _():
             own_far[e].start()
 
+    quad(0)
+
     gate_slot = slot()
-    push(gate_slot, gate_hbm.at[1 - t], gate.at[1], task_peer)
 
     @pl.when(zh == 1)
     def _():
@@ -173,61 +179,66 @@
             return w23.at[0, e // 2, y, zh, x_ // 2, lax.rem(x_, 2), c]
         return w23.at[1, e // 2, at(y, k), zh, xp, xq, c]
 
-    def a2(e, k, o, core):
-        return w1.at[e, at(y, k), plane(o), :, :, pl.ds(pl.multiple_of(512 * core, 128), 256)]
-
-    def b2(e, k, o, core):
+    def a2(e, k, o, core, rows=slice(None)):
+        return w1.at[e, at(y, k), plane(o), rows, :, pl.ds(pl.multiple_of(512 * core, 128), 256)]
+
+    def b2(e, k, o, core, rows=slice(None)):
         x_ = at(x, k)
         cols = pl.ds(pl.multiple_of(512 * core + 256 + 128 * lax.rem(x_, 2), 128), 128)
-        return w1.at[e, :, plane(o), x_ // 2, :, cols]
-
-    def c2(e, k, o, core):
+        return w1.at[e, rows, plane(o), x_ // 2, :, cols]
+
+    def c2(e, k, o, core, rows=slice(None)):
         if e % 2 == 0:
-            return w23.at[0, e // 2, at(y, k), plane(o), :, :, core]
+            return w23.at[0, e // 2, at(y, k), plane(o), rows, :, core]
         x_ = at(x, k)
-        return w23.at[1, e // 2, :, plane(o), x_ // 2, lax.rem(x_, 2), core]
+        return w23.at[1, e // 2, rows, plane(o), x_ // 2, lax.rem(x_, 2), core]
 
     class Ring:
-        def __init__(self, device, part, way):
-            self.device, self.part, self.way = device, part, way
-            self.slots = {k: slot() for k in (1, -1, 2)}
+        def __init__(self, device, part, ways):
+            self.device, self.part, self.ways = device, part, ways
+            self.slots = {k: slot() for k in (1, -1)}
+            self.far_slots = {k: slot() for k in ways}
 
         def near(self):
             for k in (1, -1):
                 push(self.slots[k], self.part(0), self.part(0), self.device(k))
 
-        def near_arrived(self):
+        def far(self):
             for k in (1, -1):
                 arrived(self.slots[k], self.part(-k))
-
-        def far(self):
-            self.near_arrived()
-            k = self.way
-            push(self.slots[2], self.part(-k), self.part(-k), self.device(k))
+            for k, half in self.ways.items():
+                push(self.far_slots[k], half(-k), half(-k), self.device(k))
 
         def far_arrived(self):
-            arrived(self.slots[2], self.part(2))
+            for k, half in self.ways.items():
+                arrived(self.far_slots[k], half(2))
 
     one, two, z_slots, shared = [], [], [], []
     for e in range(experts):
-        third = y_dev if e % 2 == 0 else x_dev
-        first_third = x_dev if e % 2 == 0 else y_dev
+        x_first, y_first = (x_dev, y_dev), (y_dev, x_dev)
         parts = [
-            (x_dev, lambda k, e=e: a1(e, k), y_dev, lambda k, o, core=c, e=e: a2(e, k, o, core)),
-            (y_dev, lambda k, e=e: b1(e, k), x_dev, lambda k, o, core=c, e=e: b2(e, k, o, core)),
-            (first_third, lambda k, e=e: c1(e, k), third, lambda k, o, core=c, e=e: c2(e, k, o, core)),
+            (x_first, lambda k, e=e: a1(e, k), functools.partial(a2, e), 2),
+            (y_first, lambda k, e=e: b1(e, k), functools.partial(b2, e), 4),
+            (x_first if e % 2 == 0 else y_first, lambda k, e=e: c1(e, k), functools.partial(c2, e), 2 if e % 2 == 0 else 4),
         ]
-        one.append([Ring(d1, p1, 1 if (e + i) % 2 == 0 else -1) for i, (d1, p1, _, _) in enumerate(parts)])
+        one.append([Ring(d[0], p1, {(1 if (e + i) % 2 == 0 else -1): p1}) for i, (d, p1, _, _) in enumerate(parts)])
         two.append([
-            [Ring(d2, lambda k, p2=p2, o=o: p2(k, o), 1 if o == 0 else -1) for _, _, d2, p2 in parts] for o in range(2)
+            [
+                Ring(d[1], lambda k, p2=p2, o=o: p2(k, o, c), {
+                    1: lambda k, p2=p2, o=o, n=n: p2(k, o, c, pl.ds(0, n // 2)),
+                    -1: lambda k, p2=p2, o=o, n=n: p2(k, o, c, pl.ds(n // 2, n // 2)),
+                })
+                for d, _, p2, n in parts
+            ]
+            for o in range(2)
         ])
         z_slots.append([slot() for _ in parts])
-        shared.append([(p2, {(k, o): slot() for k in (0, 1, -1, 2) for o in range(2)}) for _, _, _, p2 in parts])
+        shared.append([(p2, {(k, o): slot() for k in (0, 1, -1, 2) for o in range(2)}) for _, _, p2, _ in parts])
 
     def share(e, o, which):
         for part, slots in shared[e]:
             for k in which:
-                push(slots[k, o], part(k, o), part(k, o), core_peer)
+                push(slots[k, o], part(k, o, c), part(k, o, c), core_peer)
 
     def share_arrived(e):
         for part, slots in shared[e]:
@@ -248,14 +259,14 @@
     def first_done(e):
         each(one[e], "far_arrived")
         for (part, _), i in zip(shared[e], z_slots[e]):
-            push(i, part(0, 0), part(0, 0), z_peer)
+            push(i, part(0, 0, c), part(0, 0, c), z_peer)
 
     def near(e, o):
         each(two[e][o], "near")
 
     def z_done(e):
         for (part, _), i in zip(shared[e], z_slots[e]):
-            arrived(i, part(0, 1))
+            arrived(i, part(0, 1, c))
         near(e, 1)
 
     def far(e, o):
@@ -278,90 +289,119 @@
             weights[o] = jnp.exp(logits)
         numer[...] = jnp.zeros_like(numer)
 
-    eo_slots = [slot() for _ in range(experts)]
+    chunk = tokens // 3
+    eo_slots = [slot() for _ in range(experts - 1)]
+    last_slots = [slot() for _ in range(3)]
     assert used[0] <= send_sem.shape[0], used[0]
 
-    def add_up(o, e):
-        values = eo[o, e].astype(F32)
+    def add_up(o, e, rows=slice(None)):
+        values = eo[o, e, rows].astype(F32)
         for k in range(2):
-            numer[k] += weights[o, :, 2 * e + k : 2 * e + k + 1] * values
-
-    def compute(e, between=None):
-        for start in range(0, 4, 2):
-            @pl.loop(start, start + 2)
-            def _(n):
-                cols = pl.ds(pl.multiple_of(n * 256, 256), 256)
-                w = w1[e, :, :, :, :, cols].reshape(16 * 208, 256)
-                summed = jnp.dot(pooled[...], w, preferred_element_type=F32)
-                first[:, cols] = jnp.maximum(summed, 0.0).astype(BF16)
-
-            if start == 0 and between is not None:
-                between()
-
+            numer[k, rows] += weights[o, rows, 2 * e + k : 2 * e + k + 1] * values
+
+    def layer_one(e, start, stop, rows=slice(None)):
+        @pl.loop(start, stop)
+        def _(n):
+            cols = pl.ds(pl.multiple_of(n * 256, 256), 256)
+            w = w1[e, :, :, :, :, cols].reshape(16 * 208, 256)
+            summed = jnp.dot(pooled[rows], w, preferred_element_type=F32)
+            first[rows, cols] = jnp.maximum(summed, 0.0).astype(BF16)
+
+    def layers_two_three(e, rows=slice(None)):
         @pl.loop(0, 2)
         def _(n):
             cols = pl.ds(pl.multiple_of(n * 256, 256), 256)
             w = jnp.concatenate(
                 [w23[e % 2, e // 2, :, :, :, q, n, 0:64].reshape(16 * 64, 128) for q in range(2)], axis=1
             )
-            summed = jnp.dot(first[...], w, preferred_element_type=F32)
-            second[:, cols] = jnp.maximum(summed, 0.0).astype(BF16)
+            summed = jnp.dot(first[rows], w, preferred_element_type=F32)
+            second[rows, cols] = jnp.maximum(summed, 0.0).astype(BF16)
 
         w = jnp.concatenate(
             [w23[e % 2, e // 2, :, :, :, :, n, 64:80].reshape(32 * 16, 128) for n in range(2)], axis=1
         )
-        summed = jnp.dot(second[...], w, preferred_element_type=F32)
-        eo[0, e] = jnp.maximum(summed, 0.0).astype(BF16)
+        summed = jnp.dot(second[rows], w, preferred_element_type=F32)
+        eo[0, e, rows] = jnp.maximum(summed, 0.0).astype(BF16)
+
+    def compute(e, *between):
+        layer_one(e, 0, 2)
+        if between:
+            between[0]()
+        layer_one(e, 2, 4)
+        if len(between) > 1:
+            between[1]()
+        layers_two_three(e)
         push(eo_slots[e], eo.at[0, e], eo.at[1, e], task_peer)
         add_up(0, e)
 
+    def compute_last(e):
+        for i in range(3):
+            rows = pl.ds(i * chunk, chunk)
+            layer_one(e, 0, 4, rows)
+            layers_two_three(e, rows)
+            push(last_slots[i], eo.at[0, e, rows], eo.at[1, e, rows], task_peer)
+            add_up(0, e, rows)
+
+    def finish(i):
+        rows = pl.ds(i * chunk, chunk)
+        arrived(last_slots[i], eo.at[1, experts - 1, rows])
+        add_up(1, experts - 1, rows)
+        for k in range(2):
+            total = sum(weights[o, rows, 2 * e + k : 2 * e + k + 1] for o in range(2) for e in range(experts))
+            mix = (numer[k, rows] / total).astype(BF16)
+            tower = jnp.maximum(jnp.dot(mix, hidden_ref[k], preferred_element_type=F32), 0.0).astype(BF16)
+            products = tower.astype(F32) * out_w_ref[k : k + 1, :].astype(F32)
+            out_ref[rows, k : k + 1] = jnp.sum(products, axis=1, keepdims=True)
+
+    def others(e):
+        arrived(eo_slots[e], eo.at[1, e])
+        add_up(1, e)
+
     first_round(0)
-    first_round(1)
+    quad(1)
+    quad(2)
+    quad(3)
+    push(gate_slot, gate_hbm.at[1 - t], gate.at[1], task_peer)
     first_far(0)
-    first_round(2)
     first_done(0)
     near(0, 0)
+    first_round(1)
+    first_round(2)
+    first_round(3)
+    gates()
     first_far(1)
-    first_round(3)
+    first_far(2)
+    first_far(3)
     first_done(1)
     near(1, 0)
-    first_far(2)
-    gates()
     z_done(0)
+    first_done(2)
     far(0, 0)
-    first_done(2)
+    first_done(3)
     near(2, 0)
-    first_far(3)
     far(0, 1)
-    first_done(3)
     z_done(1)
     far(1, 0)
+    near(3, 0)
     far_done(0)
-    near(3, 0)
     share_arrived(0)
-    compute(0, lambda: far(1, 1))
-    z_done(2)
+    compute(0, lambda: far(1, 1), lambda: z_done(2))
     far(2, 0)
     far_done(1)
     share_arrived(1)
-    compute(1, lambda: far(2, 1))
-    z_done(3)
+    compute(1, lambda: far(2, 1), lambda: z_done(3))
     far(3, 0)
+    others(0)
     far_done(2)
     share_arrived(2)
     compute(2, lambda: far(3, 1))
+    others(1)
     far_done(3)
     share_arrived(3)
-    compute(3)
-    for e in range(experts):
-        arrived(eo_slots[e], eo.at[1, e])
-        add_up(1, e)
-
-    for k in range(2):
-        total = sum(weights[o, :, 2 * e + k : 2 * e + k + 1] for o in range(2) for e in range(experts))
-        mix = (numer[k] / total).astype(BF16)
-        tower = jnp.maximum(jnp.dot(mix, hidden_ref[k], preferred_element_type=F32), 0.0).astype(BF16)
-        out_ref[:, k : k + 1] = jnp.sum(tower.astype(F32) * out_w_ref[k : k + 1, :].astype(F32), axis=1, keepdims=True)
+    compute_last(3)
+    others(2)
+    for i in range(3):
+        finish(i)
 
     for copy in sent:
         copy.wait_send()

time: 142 us -> 132 us (0.930)
  Pallas kernels: 134 us -> 124 us
    pallas_call x1, Pallas kernels: 134 us -> 124 us  [per_device(): pl.pallas_call(kernel, out_shape=jax.ShapeDtypeStruct((tokens, 2), F32),...]
where the time goes in v3:
time: 132 us
  Pallas kernels  124 us (94%)
  local copies, waits for them, and re-layouts  6.77 us (5%)
    pallas_call x1, Pallas kernels, per_device(): pl.pallas_call(kernel, out_shape=jax.ShapeDtypeStruct((tokens, 2), F32),...  124 us

profile of v3, /device:TPU:1, one launch (start us, length us, event | category | flops | bytes accessed | tf_op | source)
XLA Modules:
  0.0 132.0 jit_solution(14223828792091564807)
XLA Ops:
  0.0 1.2 reshape.26
  1.2 0.2 copy.21
  1.4 0.3 reshape.27
  1.7 0.1 copy.15
  1.8 0.9 copy.13
  2.6 0.7 reshape.30
  3.4 0.9 pad_maximum_fusion.block_hbm
  4.2 0.9 reshape.32
  5.2 0.1 copy.22
  5.3 0.7 reshape.33.gate_hbm
  6.0 124.3 %shard_map.73 = f32[768,2]{1,0:T(8,128)} custom-call(bf16[768,3328]{1,0:T(8,128)(2,1)} %pooled_hbm.1, bf16[4,4,64,256]{3,2,1,0:T(8,128)(2,1)} %pad_maximum_fusion.block_hbm, bf16[2,8,3328]{2,1,0:T(8,128)(2,1)} %reshape.33.gate_hbm, bf16[2,256,128]{2,1,0:T(8,128)(2,1)} %hidden_ref.1, bf16[2,128]{1,0:T(2,128)(2,1)} %out_w_ref.1), custom_call_target="tpu_custom_call" | custom-call | tf_op jit(solution)/shard_map/pallas_call | solution.py:421
  130.2 1.7 %copy.17 = f32[768,2]{0,1:T(2,128)} copy(f32[768,2]{1,0:T(8,128)} %shard_map.73) | data formatting | bytes 12288 | tf_op jit(solution)/shard_map/pallas_call | solution.py:421
  (2 shorter events, 0.0 us)

commit v4 on v3

--- a/solution.py
+++ b/solution.py
@@ -30,8 +30,8 @@
 
 
 def kernel(
-    pooled_hbm, block_hbm, gate_hbm, hidden_ref, out_w_ref, out_ref,
-    staged, w1, w23, pooled, gate, first, second, eo, numer, weights, send_sem, recv_sem, local_sem,
+    pooled_hbm, gate_hbm, first_hbm, second_hbm, third_hbm, hidden_ref, out_w_ref, out_ref,
+    raw1, raw2, raw3, block, staged, w1, w23, pooled, gate, first, second, eo, numer, weights, send_sem, recv_sem, local_sem,
 ):
     t, y, zh, x, c = (lax.axis_index(a) for a in AXES)
     xp, xq = x // 2, lax.rem(x, 2)
@@ -75,23 +75,51 @@
         ).wait_recv()
 
     half = tokens // 2
+    shards = [
+        pltpu.make_async_copy(src, dst, local_sem.at[i])
+        for i, (src, dst) in enumerate([(first_hbm, raw1), (second_hbm, raw2), (third_hbm, raw3)])
+    ]
     loads = [
-        pltpu.make_async_copy(pooled_hbm.at[pl.ds(k * half, half)], pooled.at[pl.ds(k * half, half)], local_sem.at[k])
+        pltpu.make_async_copy(pooled_hbm.at[pl.ds(k * half, half)], pooled.at[pl.ds(k * half, half)], local_sem.at[3 + k])
         for k in range(2)
     ]
-    loads.append(pltpu.make_async_copy(gate_hbm.at[t], gate.at[0], local_sem.at[2]))
-    own_block = pltpu.make_async_copy(block_hbm.at[j], staged.at[j], local_sem.at[3])
-    for load in loads:
+    loads.append(pltpu.make_async_copy(gate_hbm, gate.at[0], local_sem.at[5]))
+    for load in shards + loads:
         load.start()
-
-    @pl.when(zh == 1)
-    def _():
-        own_block.start()
 
     barrier = pltpu.get_barrier_semaphore()
     peers = [x_dev(1), x_dev(-1), y_dev(1), y_dev(-1), z_peer, core_peer, task_peer] + [quad_dev(d) for d in range(1, QUAD)]
     for device in peers:
         pl.semaphore_signal(barrier, inc=1, device_id=device, device_id_type=MESH)
+
+    for load in shards:
+        load.wait()
+
+    def place(rows, columns, source):
+        row = lax.broadcasted_iota(jnp.int32, (rows, columns), 0)
+        column = lax.broadcasted_iota(jnp.int32, (rows, columns), 1)
+        return jnp.where(source(row) == column, 1.0, 0.0).astype(BF16)
+
+    def band(row, start, size, source):
+        return jnp.where((row >= start) & (row < start + size), source, -1)
+
+    def build(e):
+        put1 = place(BLOCK, experts * W1_ROWS, lambda r: band(r, 0, W1_ROWS, experts * r + e))
+        rows1 = jnp.dot(put1, raw1[...].reshape(experts * W1_ROWS, 1024), preferred_element_type=F32)
+        rows2, rows3 = [], []
+        for side in range(2):
+            put2 = place(BLOCK, 16, lambda r: band(r, W1_ROWS, W2_ROWS, r - W1_ROWS + W2_ROWS * side))
+            put3 = place(BLOCK, 8, lambda r: band(r, W1_ROWS + W2_ROWS, W3_ROWS, r - W1_ROWS - W2_ROWS + W3_ROWS * side))
+            rows2.append(jnp.dot(put2, raw2[e], preferred_element_type=F32))
+            rows3.append(jnp.dot(put3, raw3[e], preferred_element_type=F32))
+        for member in range(QUAD):
+            q, n = member // 2, member % 2
+            for side in range(2):
+                col1, col2, col3 = 512 * n + 256 * side + 128 * q, 256 * n + 128 * q, 128 * n
+                both = rows1[:, col1 : col1 + 128] + rows2[side][:, col2 : col2 + 128] + rows3[side][:, col3 : col3 + 128]
+                block[member, e, :, 128 * side : 128 * side + 128] = both.astype(BF16)
+
+    build(0)
     pl.semaphore_wait(barrier, len(peers))
 
     def member(d):
@@ -100,7 +128,7 @@
     quad_slots = [[slot() for _ in range(QUAD)] for _ in range(experts)]
     own_far = [
         pltpu.make_async_remote_copy(
-            src_ref=block_hbm.at[j, e], dst_ref=staged.at[j, e], send_sem=send_sem.at[quad_slots[e][0]],
+            src_ref=block.at[j, e], dst_ref=staged.at[j, e], send_sem=send_sem.at[quad_slots[e][0]],
             recv_sem=recv_sem.at[quad_slots[e][0]], device_id=task_peer, device_id_type=MESH,
         )
         for e in range(experts)
@@ -108,19 +136,20 @@
 
     def quad(e):
         for d in range(1, QUAD):
-            push(quad_slots[e][d], block_hbm.at[member(d), e], staged.at[j, e], quad_dev(d))
+            push(quad_slots[e][d], block.at[member(d), e], staged.at[j, e], quad_dev(d))
 
         @pl.when(zh == 0)
         def _():
             own_far[e].start()
 
+        @pl.when(zh == 1)
+        def _():
+            staged[j, e] = block[j, e]
+
     quad(0)
-
+    for e in range(1, experts):
+        build(e)
     gate_slot = slot()
-
-    @pl.when(zh == 1)
-    def _():
-        own_block.wait()
 
     def w1_source(r):
         return r + (BLOCK - W1_ROWS) * (
@@ -284,9 +313,11 @@
         arrived(gate_slot, gate.at[1])
         own_gate = jnp.where(zh == 1, 0, 1)
         for o in range(2):
-            g = gate[own_gate if o == 0 else 1 - own_gate]
+            g = gate[own_gate if o == 0 else 1 - own_gate].reshape(4 * experts, pooled.shape[1])
             logits = lax.dot_general(pooled[...], g, (((1,), (1,)), ((), ())), preferred_element_type=F32)
-            weights[o] = jnp.exp(logits)
+            for e in range(experts):
+                own = jnp.where(t == 0, logits[:, 4 * e : 4 * e + 2], logits[:, 4 * e + 2 : 4 * e + 4])
+                weights[o, :, 2 * e : 2 * e + 2] = jnp.exp(own)
         numer[...] = jnp.zeros_like(numer)
 
     chunk = tokens // 3
@@ -350,8 +381,9 @@
             total = sum(weights[o, rows, 2 * e + k : 2 * e + k + 1] for o in range(2) for e in range(experts))
             mix = (numer[k, rows] / total).astype(BF16)
             tower = jnp.maximum(jnp.dot(mix, hidden_ref[k], preferred_element_type=F32), 0.0).astype(BF16)
-            products = tower.astype(F32) * out_w_ref[k : k + 1, :].astype(F32)
-            out_ref[rows, k : k + 1] = jnp.sum(products, axis=1, keepdims=True)
+            out_ref[k : k + 1, rows] = lax.dot_general(
+                out_w_ref[k : k + 1, :], tower, (((1,), (1,)), ((), ())), preferred_element_type=F32
+            )
 
     def others(e):
         arrived(eo_slots[e], eo.at[1, e])
@@ -361,7 +393,7 @@
     quad(1)
     quad(2)
     quad(3)
-    push(gate_slot, gate_hbm.at[1 - t], gate.at[1], task_peer)
+    push(gate_slot, gate_hbm, gate.at[1], task_peer)
     first_far(0)
     first_done(0)
     near(0, 0)
@@ -410,25 +442,23 @@
 def per_device(pooled, gate_weight, w_first, w_second, w_third, tower_hidden, tower_out):
     tokens, width = pooled.shape
     experts = w_first.shape[0]
-    one = w_first.reshape(experts, 52, 2, 2, 2, 128).transpose(4, 2, 0, 1, 3, 5).reshape(4, experts, 52, 256)
-    two = w_second.reshape(experts, 2, 8, 2, 2, 128).transpose(4, 3, 0, 2, 1, 5).reshape(4, experts, 8, 256)
-    three = w_third.reshape(experts, 2, 4, 2, 128).transpose(3, 0, 2, 1, 4).reshape(1, 2, experts, 4, 256)
-    three = jnp.broadcast_to(three, (2, 2, experts, 4, 256)).reshape(4, experts, 4, 256)
-    block = jnp.concatenate([one, two, three], axis=2)
-    gate = gate_weight.reshape(width, experts, 2, 2).transpose(2, 1, 3, 0).reshape(2, 2 * experts, width)
     any_, vmem = pl.BlockSpec(memory_space=pl.ANY), pl.BlockSpec(memory_space=pltpu.VMEM)
     slots = 300
     return pl.pallas_call(
         kernel,
-        out_shape=jax.ShapeDtypeStruct((tokens, 2), F32),
-        in_specs=[any_, any_, any_, vmem, vmem],
+        out_shape=jax.ShapeDtypeStruct((2, tokens), F32),
+        in_specs=[any_] * 5 + [vmem, vmem],
         out_specs=vmem,
         scratch_shapes=[
+            pltpu.VMEM((52, experts, 1024), BF16),
+            pltpu.VMEM((experts, 16, 512), BF16),
+            pltpu.VMEM((experts, 8, 256), BF16),
+            pltpu.VMEM((QUAD, experts, BLOCK, 256), BF16),
             pltpu.VMEM((QUAD, experts, BLOCK, 256), BF16),
             pltpu.VMEM((experts, 4, 2, 2, 208, 1024), BF16),
             pltpu.VMEM((2, 2, 4, 2, 2, 2, 2, 80, 128), BF16),
             pltpu.VMEM((tokens, width), BF16),
-            pltpu.VMEM((2, 2 * experts, width), BF16),
+            pltpu.VMEM((2, experts, 4, width), BF16),
             pltpu.VMEM((tokens, 1024), BF16),
             pltpu.VMEM((tokens, 512), BF16),
             pltpu.VMEM((2, experts, tokens, 256), BF16),
@@ -436,12 +466,14 @@
             pltpu.VMEM((2, tokens, 2 * experts), F32),
             pltpu.SemaphoreType.DMA((slots,)),
             pltpu.SemaphoreType.DMA((slots,)),
-            pltpu.SemaphoreType.DMA((4,)),
+            pltpu.SemaphoreType.DMA((6,)),
         ],
         compiler_params=pltpu.CompilerParams(
             collective_id=0, has_side_effects=True, vmem_limit_bytes=67_000_000
         ),
-    )(pooled, block, gate, tower_hidden, tower_out)
+    )(
+        pooled, gate_weight.transpose(1, 2, 0), w_first.transpose(1, 0, 2), w_second, w_third, tower_hidden, tower_out
+    ).T
 
 
 def solution(mesh):

time: 132 us -> 125 us (0.947)
  local copies, waits for them, and re-layouts: 6.77 us -> 1.29 us
    reshape x10 -> x0, local copies, waits for them, and re-layouts: 5.02 us -> none  [the longest x4 1.73 us: per_device(): w_first.reshape(experts, 52, 2, 2, 2, 128).transpose(4, 2, 0, 1, 3, 5)]
    pallas_call x1 -> x0, local copies, waits for them, and re-layouts: 1.74 us -> none  [per_device(): pl.pallas_call(kernel, out_shape=jax.ShapeDtypeStruct((tokens, 2), F32),...]
where the time goes in v4:
time: 125 us
  Pallas kernels  124 us (99%)
  local copies, waits for them, and re-layouts  1.29 us (1%)
    pallas_call x1, Pallas kernels, per_device(): pl.pallas_call(kernel, out_shape=jax.ShapeDtypeStruct((2, tokens), F32),...  124 us

profile of v4, /device:TPU:1, one launch (start us, length us, event | category | flops | bytes accessed | tf_op | source)
XLA Modules:
  0.0 125.0 jit_solution(5963274333810984508)
XLA Ops:
  0.0 123.7 %shard_map.73 = f32[2,768]{1,0:T(2,128)} custom-call(bf16[768,3328]{1,0:T(8,128)(2,1)} %pooled_hbm.1, bf16[4,4,3328]{2,1,0:T(4,128)(2,1)} %bitcast.4, bf16[52,4,1024]{2,1,0:T(4,128)(2,1)} %bitcast.3, bf16[4,16,512]{2,1,0:T(8,128)(2,1)} %second_hbm.1, bf16[4,8,256]{2,1,0:T(8,128)(2,1)} %third_hbm.1, bf16[2,256,128]{2,1,0:T(8,128)(2,1)} %hidden_ref.1, ...), custom_call_target="tpu_custom_call" | custom-call | tf_op jit(solution)/shard_map/pallas_call | solution.py:447
  123.7 1.3 %copy.9 = f32[768,2]{0,1:T(2,128)} copy(f32[768,2]{0,1:T(2,128)} %bitcast.5) | data formatting | bytes 12288

commit v5 on v4

--- a/solution.py
+++ b/solution.py
@@ -88,7 +88,7 @@
         load.start()
 
     barrier = pltpu.get_barrier_semaphore()
-    peers = [x_dev(1), x_dev(-1), y_dev(1), y_dev(-1), z_peer, core_peer, task_peer] + [quad_dev(d) for d in range(1, QUAD)]
+    peers = [x_dev(1), x_dev(-1), x_dev(2), y_dev(1), y_dev(-1), y_dev(2), z_peer, core_peer, task_peer] + [quad_dev(d) for d in range(1, QUAD)]
     for device in peers:
         pl.semaphore_signal(barrier, inc=1, device_id=device, device_id_type=MESH)
 
@@ -223,18 +223,24 @@
         return w23.at[1, e // 2, rows, plane(o), x_ // 2, lax.rem(x_, 2), core]
 
     class Ring:
-        def __init__(self, device, part, ways):
-            self.device, self.part, self.ways = device, part, ways
+        def __init__(self, device, part, ways, direct=False):
+            self.device, self.part, self.ways, self.direct = device, part, ways, direct
             self.slots = {k: slot() for k in (1, -1)}
             self.far_slots = {k: slot() for k in ways}
 
         def near(self):
             for k in (1, -1):
                 push(self.slots[k], self.part(0), self.part(0), self.device(k))
-
-        def far(self):
+            if self.direct:
+                for k in self.ways:
+                    push(self.far_slots[k], self.part(0), self.part(0), self.device(2))
+
+        def near_arrived(self):
             for k in (1, -1):
                 arrived(self.slots[k], self.part(-k))
+
+        def far(self):
+            self.near_arrived()
             for k, half in self.ways.items():
                 push(self.far_slots[k], half(-k), half(-k), self.device(k))
 
@@ -250,7 +256,7 @@
             (y_first, lambda k, e=e: b1(e, k), functools.partial(b2, e), 4),
             (x_first if e % 2 == 0 else y_first, lambda k, e=e: c1(e, k), functools.partial(c2, e), 2 if e % 2 == 0 else 4),
         ]
-        one.append([Ring(d[0], p1, {(1 if (e + i) % 2 == 0 else -1): p1}) for i, (d, p1, _, _) in enumerate(parts)])
+        one.append([Ring(d[0], p1, {(1 if (e + i) % 2 == 0 else -1): p1}, e < 1) for i, (d, p1, _, _) in enumerate(parts)])
         two.append([
             [
                 Ring(d[1], lambda k, p2=p2, o=o: p2(k, o, c), {
@@ -286,6 +292,8 @@
         each(one[e], "far")
 
     def first_done(e):
+        if e < 1:
+            each(one[e], "near_arrived")
         each(one[e], "far_arrived")
         for (part, _), i in zip(shared[e], z_slots[e]):
             push(i, part(0, 0, c), part(0, 0, c), z_peer)
@@ -298,27 +306,36 @@
             arrived(i, part(0, 1, c))
         near(e, 1)
 
+    far_by_z = {e: [slot() for _ in range(3)] for e in (2,)}
+
     def far(e, o):
-        each(two[e][o], "far")
-        share(e, o, (0, 1, -1))
-
-    def far_done(e):
-        for o in range(2):
+        each(two[e][o], "near_arrived" if o == 1 and e in far_by_z else "far")
+
+    def far_done(e, o):
+        if o == 1 and e in far_by_z:
+            for (part, _), i in zip(shared[e], far_by_z[e]):
+                arrived(i, part(2, 1, c))
+        else:
             each(two[e][o], "far_arrived")
-            share(e, o, (2,))
-
-    def gates():
-        for load in loads:
-            load.wait()
-        arrived(gate_slot, gate.at[1])
-        own_gate = jnp.where(zh == 1, 0, 1)
-        for o in range(2):
-            g = gate[own_gate if o == 0 else 1 - own_gate].reshape(4 * experts, pooled.shape[1])
-            logits = lax.dot_general(pooled[...], g, (((1,), (1,)), ((), ())), preferred_element_type=F32)
+        if o == 0 and e in far_by_z:
+            for (part, _), i in zip(shared[e], far_by_z[e]):
+                push(i, part(2, 0, c), part(2, 0, c), z_peer)
+
+    def gates(o):
+        if o == 0:
+            for load in loads:
+                load.wait()
+            numer[...] = jnp.zeros_like(numer)
+        else:
+            arrived(gate_slot, gate.at[1])
+        side = jnp.where(zh == 1, o, 1 - o)
+        g = gate[o].reshape(4 * experts, pooled.shape[1])
+        for part in range(2):
+            rows = pl.ds(part * half, half)
+            logits = lax.dot_general(pooled[rows], g, (((1,), (1,)), ((), ())), preferred_element_type=F32)
             for e in range(experts):
                 own = jnp.where(t == 0, logits[:, 4 * e : 4 * e + 2], logits[:, 4 * e + 2 : 4 * e + 4])
-                weights[o, :, 2 * e : 2 * e + 2] = jnp.exp(own)
-        numer[...] = jnp.zeros_like(numer)
+                weights[side, rows, 2 * e : 2 * e + 2] = jnp.exp(own)
 
     chunk = tokens // 3
     eo_slots = [slot() for _ in range(experts - 1)]
@@ -330,37 +347,30 @@
         for k in range(2):
             numer[k, rows] += weights[o, rows, 2 * e + k : 2 * e + k + 1] * values
 
-    def layer_one(e, start, stop, rows=slice(None)):
-        @pl.loop(start, stop)
-        def _(n):
-            cols = pl.ds(pl.multiple_of(n * 256, 256), 256)
+    def layer_one(e, h, rows=slice(None)):
+        for n in (2 * h, 2 * h + 1):
+            cols = slice(256 * n, 256 * n + 256)
             w = w1[e, :, :, :, :, cols].reshape(16 * 208, 256)
             summed = jnp.dot(pooled[rows], w, preferred_element_type=F32)
             first[rows, cols] = jnp.maximum(summed, 0.0).astype(BF16)
 
-    def layers_two_three(e, rows=slice(None)):
-        @pl.loop(0, 2)
-        def _(n):
-            cols = pl.ds(pl.multiple_of(n * 256, 256), 256)
+    def layers_two_three(e, start=0, size=tokens):
+        rows = pl.ds(start, size)
+        for n in range(2):
             w = jnp.concatenate(
                 [w23[e % 2, e // 2, :, :, :, q, n, 0:64].reshape(16 * 64, 128) for q in range(2)], axis=1
             )
             summed = jnp.dot(first[rows], w, preferred_element_type=F32)
-            second[rows, cols] = jnp.maximum(summed, 0.0).astype(BF16)
-
+            second[rows, 256 * n : 256 * n + 256] = jnp.maximum(summed, 0.0).astype(BF16)
         w = jnp.concatenate(
             [w23[e % 2, e // 2, :, :, :, :, n, 64:80].reshape(32 * 16, 128) for n in range(2)], axis=1
         )
-        summed = jnp.dot(second[rows], w, preferred_element_type=F32)
-        eo[0, e, rows] = jnp.maximum(summed, 0.0).astype(BF16)
-
-    def compute(e, *between):
-        layer_one(e, 0, 2)
-        if between:
-            between[0]()
-        layer_one(e, 2, 4)
-        if len(between) > 1:
-            between[1]()
+        for part in range(2):
+            rows = pl.ds(start + part * (size // 2), size // 2)
+            summed = jnp.dot(second[rows], w, preferred_element_type=F32)
+            eo[0, e, rows] = jnp.maximum(summed, 0.0).astype(BF16)
+
+    def expert_done(e):
         layers_two_three(e)
         push(eo_slots[e], eo.at[0, e], eo.at[1, e], task_peer)
         add_up(0, e)
@@ -368,8 +378,9 @@
     def compute_last(e):
         for i in range(3):
             rows = pl.ds(i * chunk, chunk)
-            layer_one(e, 0, 4, rows)
-            layers_two_three(e, rows)
+            for h in range(2):
+                layer_one(e, h, rows)
+            layers_two_three(e, i * chunk, chunk)
             push(last_slots[i], eo.at[0, e, rows], eo.at[1, e, rows], task_peer)
             add_up(0, e, rows)
 
@@ -389,46 +400,85 @@
         arrived(eo_slots[e], eo.at[1, e])
         add_up(1, e)
 
+    gates(0)
     first_round(0)
     quad(1)
+    push(gate_slot, gate_hbm, gate.at[1], task_peer)
+    first_round(1)
     quad(2)
     quad(3)
-    push(gate_slot, gate_hbm, gate.at[1], task_peer)
-    first_far(0)
     first_done(0)
     near(0, 0)
-    first_round(1)
     first_round(2)
+    first_far(1)
     first_round(3)
-    gates()
-    first_far(1)
+    far(0, 0)
+    gates(1)
+    share(0, 0, (1, -1))
+    first_done(1)
+    share(0, 0, (0,))
+    near(1, 0)
     first_far(2)
     first_far(3)
-    first_done(1)
-    near(1, 0)
     z_done(0)
+    far(1, 0)
+    far_done(0, 0)
+    share(1, 0, (0,))
+    first_done(3)
     first_done(2)
-    far(0, 0)
-    first_done(3)
+    share(0, 1, (0,))
     near(2, 0)
+    share(0, 0, (2,))
+    z_done(1)
+    far_done(1, 0)
     far(0, 1)
-    z_done(1)
-    far(1, 0)
+    share(1, 1, (0,))
+    far(2, 0)
+    share(0, 1, (1, -1))
+    far(1, 1)
+    share(1, 0, (2,))
+    share(3, 0, (0,))
     near(3, 0)
-    far_done(0)
+    share(1, 1, (1, -1))
+    far_done(0, 1)
+    share(0, 1, (2,))
+    z_done(2)
+    share(1, 0, (1, -1))
+    share(2, 0, (0,))
+    far_done(2, 0)
+    share(2, 0, (2,))
     share_arrived(0)
-    compute(0, lambda: far(1, 1), lambda: z_done(2))
-    far(2, 0)
-    far_done(1)
+    share(2, 0, (1, -1))
+    layer_one(0, 0)
+    layer_one(0, 1)
+    far_done(1, 1)
+    z_done(3)
+    share(1, 1, (2,))
+    expert_done(0)
+    far(3, 0)
+    share(3, 0, (1, -1))
+    share(2, 1, (0,))
+    share(3, 1, (0,))
     share_arrived(1)
-    compute(1, lambda: far(2, 1), lambda: z_done(3))
-    far(3, 0)
+    layer_one(1, 0)
+    layer_one(1, 1)
+    far(2, 1)
+    share(2, 1, (1, -1))
+    far_done(2, 1)
+    share(2, 1, (2,))
+    expert_done(1)
     others(0)
-    far_done(2)
+    far(3, 1)
+    share(3, 1, (1, -1))
     share_arrived(2)
-    compute(2, lambda: far(3, 1))
+    layer_one(2, 0)
+    far_done(3, 0)
+    layer_one(2, 1)
+    share(3, 0, (2,))
+    far_done(3, 1)
+    share(3, 1, (2,))
+    expert_done(2)
     others(1)
-    far_done(3)
     share_arrived(3)
     compute_last(3)
     others(2)

time: 125 us -> 119 us (0.952)
  Pallas kernels: 124 us -> 117 us
    pallas_call x1, Pallas kernels: 124 us -> 117 us  [per_device(): pl.pallas_call(kernel, out_shape=jax.ShapeDtypeStruct((2, tokens), F32),...]
where the time goes in v5:
time: 119 us
  Pallas kernels  117 us (98%)
  local copies, waits for them, and re-layouts  1.29 us (1%)
    pallas_call x1, Pallas kernels, per_device(): pl.pallas_call(kernel, out_shape=jax.ShapeDtypeStruct((2, tokens), F32),...  117 us

profile of v5, /device:TPU:1, one launch (start us, length us, event | category | flops | bytes accessed | tf_op | source)
XLA Modules:
  0.0 118.5 jit_solution(14444187117720739932)
XLA Ops:
  0.0 117.2 %shard_map.73 = f32[2,768]{1,0:T(2,128)} custom-call(bf16[768,3328]{1,0:T(8,128)(2,1)} %pooled_hbm.1, bf16[4,4,3328]{2,1,0:T(4,128)(2,1)} %bitcast.4, bf16[52,4,1024]{2,1,0:T(4,128)(2,1)} %bitcast.3, bf16[4,16,512]{2,1,0:T(8,128)(2,1)} %second_hbm.1, bf16[4,8,256]{2,1,0:T(8,128)(2,1)} %third_hbm.1, bf16[2,256,128]{2,1,0:T(8,128)(2,1)} %hidden_ref.1, ...), custom_call_target="tpu_custom_call" | custom-call | tf_op jit(solution)/shard_map/pallas_call | solution.py:497
  117.2 1.3 %copy.9 = f32[768,2]{0,1:T(2,128)} copy(f32[768,2]{0,1:T(2,128)} %bitcast.5) | data formatting | bytes 12288

commit v6 on v5

--- a/solution.py
+++ b/solution.py
@@ -338,8 +338,7 @@
                 weights[side, rows, 2 * e : 2 * e + 2] = jnp.exp(own)
 
     chunk = tokens // 3
-    eo_slots = [slot() for _ in range(experts - 1)]
-    last_slots = [slot() for _ in range(3)]
+    eo_slots = [[slot() for _ in range(3)] for _ in range(experts)]
     assert used[0] <= send_sem.shape[0], used[0]
 
     def add_up(o, e, rows=slice(None)):
@@ -370,23 +369,22 @@
             summed = jnp.dot(second[rows], w, preferred_element_type=F32)
             eo[0, e, rows] = jnp.maximum(summed, 0.0).astype(BF16)
 
-    def expert_done(e):
-        layers_two_three(e)
-        push(eo_slots[e], eo.at[0, e], eo.at[1, e], task_peer)
-        add_up(0, e)
-
-    def compute_last(e):
+    def compute(e, i):
+        rows = pl.ds(i * chunk, chunk)
+        for h in range(2):
+            layer_one(e, h, rows)
+        layers_two_three(e, i * chunk, chunk)
+        push(eo_slots[e][i], eo.at[0, e, rows], eo.at[1, e, rows], task_peer)
+        add_up(0, e, rows)
+
+    def others(e):
         for i in range(3):
-            rows = pl.ds(i * chunk, chunk)
-            for h in range(2):
-                layer_one(e, h, rows)
-            layers_two_three(e, i * chunk, chunk)
-            push(last_slots[i], eo.at[0, e, rows], eo.at[1, e, rows], task_peer)
-            add_up(0, e, rows)
+            arrived(eo_slots[e][i], eo.at[1, e, pl.ds(i * chunk, chunk)])
+        add_up(1, e)
 
     def finish(i):
         rows = pl.ds(i * chunk, chunk)
-        arrived(last_slots[i], eo.at[1, experts - 1, rows])
+        arrived(eo_slots[experts - 1][i], eo.at[1, experts - 1, rows])
         add_up(1, experts - 1, rows)
         for k in range(2):
             total = sum(weights[o, rows, 2 * e + k : 2 * e + k + 1] for o in range(2) for e in range(experts))
@@ -396,92 +394,90 @@
                 out_w_ref[k : k + 1, :], tower, (((1,), (1,)), ((), ())), preferred_element_type=F32
             )
 
-    def others(e):
-        arrived(eo_slots[e], eo.at[1, e])
-        add_up(1, e)
-
     gates(0)
+    quad(1)
     first_round(0)
-    quad(1)
-    push(gate_slot, gate_hbm, gate.at[1], task_peer)
+    quad(2)
     first_round(1)
-    quad(2)
     quad(3)
+    first_round(2)
+    first_round(3)
     first_done(0)
+    first_far(1)
     near(0, 0)
-    first_round(2)
-    first_far(1)
-    first_round(3)
-    far(0, 0)
-    gates(1)
-    share(0, 0, (1, -1))
-    first_done(1)
-    share(0, 0, (0,))
-    near(1, 0)
     first_far(2)
     first_far(3)
+    first_done(1)
+    near(1, 0)
+    first_done(2)
     z_done(0)
+    push(gate_slot, gate_hbm, gate.at[1], task_peer)
+    near(2, 0)
+    far(0, 1)
     far(1, 0)
+    share(1, 0, (1, -1))
+    z_done(1)
+    far(0, 0)
+    far(2, 0)
+    first_done(3)
+    share(0, 0, (1, -1))
+    far_done(0, 1)
+    share(0, 1, (0,))
+    share(2, 0, (0,))
+    far_done(1, 0)
+    far(1, 1)
+    z_done(2)
+    share(0, 1, (1, -1))
+    share(2, 1, (0,))
+    share(0, 0, (0,))
     far_done(0, 0)
-    share(1, 0, (0,))
-    first_done(3)
-    first_done(2)
-    share(0, 1, (0,))
-    near(2, 0)
     share(0, 0, (2,))
-    z_done(1)
-    far_done(1, 0)
-    far(0, 1)
+    near(3, 0)
+    share(0, 1, (2,))
+    gates(1)
+    share(2, 0, (1, -1))
     share(1, 1, (0,))
-    far(2, 0)
-    share(0, 1, (1, -1))
-    far(1, 1)
+    share_arrived(0)
     share(1, 0, (2,))
-    share(3, 0, (0,))
-    near(3, 0)
-    share(1, 1, (1, -1))
-    far_done(0, 1)
-    share(0, 1, (2,))
-    z_done(2)
-    share(1, 0, (1, -1))
-    share(2, 0, (0,))
+    z_done(3)
     far_done(2, 0)
     share(2, 0, (2,))
-    share_arrived(0)
-    share(2, 0, (1, -1))
-    layer_one(0, 0)
-    layer_one(0, 1)
+    share(1, 1, (1, -1))
+    share(3, 1, (0,))
+    share(1, 0, (0,))
+    compute(0, 0)
+    share(3, 0, (0,))
     far_done(1, 1)
-    z_done(3)
     share(1, 1, (2,))
-    expert_done(0)
+    compute(0, 1)
+    compute(0, 2)
+    far(2, 1)
+    share_arrived(1)
+    compute(1, 0)
+    compute(1, 1)
+    far_done(2, 1)
+    share(2, 1, (1, -1))
     far(3, 0)
-    share(3, 0, (1, -1))
-    share(2, 1, (0,))
-    share(3, 1, (0,))
-    share_arrived(1)
-    layer_one(1, 0)
-    layer_one(1, 1)
-    far(2, 1)
-    share(2, 1, (1, -1))
-    far_done(2, 1)
     share(2, 1, (2,))
-    expert_done(1)
+    compute(1, 2)
     others(0)
     far(3, 1)
+    share_arrived(2)
     share(3, 1, (1, -1))
-    share_arrived(2)
-    layer_one(2, 0)
+    compute(2, 0)
+    share(3, 0, (1, -1))
     far_done(3, 0)
-    layer_one(2, 1)
     share(3, 0, (2,))
+    compute(2, 1)
     far_done(3, 1)
     share(3, 1, (2,))
-    expert_done(2)
+    compute(2, 2)
+    share_arrived(3)
+    compute(3, 0)
+    compute(3, 1)
     others(1)
-    share_arrived(3)
-    compute_last(3)
     others(2)
+    compute(3, 2)
     for i in range(3):
         finish(i)
 

time: 119 us -> 114 us (0.958)
  Pallas kernels: 117 us -> 112 us
    pallas_call x1, Pallas kernels: 117 us -> 112 us  [per_device(): pl.pallas_call(kernel, out_shape=jax.ShapeDtypeStruct((2, tokens), F32),...]
where the time goes in v6:
time: 114 us
  Pallas kernels  112 us (98%)
  local copies, waits for them, and re-layouts  1.29 us (1%)
    pallas_call x1, Pallas kernels, per_device(): pl.pallas_call(kernel, out_shape=jax.ShapeDtypeStruct((2, tokens), F32),...  112 us

profile of v6, /device:TPU:1, one launch (start us, length us, event | category | flops | bytes accessed | tf_op | source)
XLA Modules:
  0.0 113.7 jit_solution(17220904045445529503)
XLA Ops:
  0.0 112.4 %shard_map.73 = f32[2,768]{1,0:T(2,128)} custom-call(bf16[768,3328]{1,0:T(8,128)(2,1)} %pooled_hbm.1, bf16[4,4,3328]{2,1,0:T(4,128)(2,1)} %bitcast.4, bf16[52,4,1024]{2,1,0:T(4,128)(2,1)} %bitcast.3, bf16[4,16,512]{2,1,0:T(8,128)(2,1)} %second_hbm.1, bf16[4,8,256]{2,1,0:T(8,128)(2,1)} %third_hbm.1, bf16[2,256,128]{2,1,0:T(8,128)(2,1)} %hidden_ref.1, ...), custom_call_target="tpu_custom_call" | custom-call | tf_op jit(solution)/shard_map/pallas_call | solution.py:493
  112.4 1.3 %copy.9 = f32[768,2]{0,1:T(2,128)} copy(f32[768,2]{0,1:T(2,128)} %bitcast.5) | data formatting | bytes 12288

commit v7 on v6

--- a/solution.py
+++ b/solution.py
@@ -31,7 +31,7 @@
 
 def kernel(
     pooled_hbm, gate_hbm, first_hbm, second_hbm, third_hbm, hidden_ref, out_w_ref, out_ref,
-    raw1, raw2, raw3, block, staged, w1, w23, pooled, gate, first, second, eo, numer, weights, send_sem, recv_sem, local_sem,
+    raw1, raw2, raw3, block, staged, w1, w23, pooled, gate, first, second, partial, eo, numer, weights, send_sem, recv_sem, local_sem,
 ):
     t, y, zh, x, c = (lax.axis_index(a) for a in AXES)
     xp, xq = x // 2, lax.rem(x, 2)
@@ -256,7 +256,7 @@
             (y_first, lambda k, e=e: b1(e, k), functools.partial(b2, e), 4),
             (x_first if e % 2 == 0 else y_first, lambda k, e=e: c1(e, k), functools.partial(c2, e), 2 if e % 2 == 0 else 4),
         ]
-        one.append([Ring(d[0], p1, {(1 if (e + i) % 2 == 0 else -1): p1}, e < 1) for i, (d, p1, _, _) in enumerate(parts)])
+        one.append([Ring(d[0], p1, {(1 if (e + i) % 2 == 0 else -1): p1}, e < 2) for i, (d, p1, _, _) in enumerate(parts)])
         two.append([
             [
                 Ring(d[1], lambda k, p2=p2, o=o: p2(k, o, c), {
@@ -275,10 +275,10 @@
             for k in which:
                 push(slots[k, o], part(k, o, c), part(k, o, c), core_peer)
 
-    def share_arrived(e):
+    def share_arrived(e, o):
         for part, slots in shared[e]:
-            for (k, o), i in slots.items():
-                arrived(i, part(k, o, 1 - c))
+            for k in (0, 1, -1, 2):
+                arrived(slots[k, o], part(k, o, 1 - c))
 
     def each(rings, step):
         for ring in rings:
@@ -292,7 +292,7 @@
         each(one[e], "far")
 
     def first_done(e):
-        if e < 1:
+        if e < 2:
             each(one[e], "near_arrived")
         each(one[e], "far_arrived")
         for (part, _), i in zip(shared[e], z_slots[e]):
@@ -346,11 +346,31 @@
         for k in range(2):
             numer[k, rows] += weights[o, rows, 2 * e + k : 2 * e + k + 1] * values
 
+    def by_plane():
+        run, rows_each = 2 * 208, tokens // 12
+
+        @pl.loop(0, 12)
+        def _(i):
+            rows = pl.ds(pl.multiple_of(i * rows_each, rows_each), rows_each)
+            values = pooled[rows]
+            pooled[rows] = jnp.concatenate(
+                [values[:, (2 * n + p) * run : (2 * n + p + 1) * run] for p in range(2) for n in range(4)], axis=1
+            )
+
+    def plane_sum(e, o, n, rows):
+        p = plane(o)
+        depth = 8 * 208
+        w = w1[e, :, p, :, :, 256 * n : 256 * n + 256].reshape(depth, 256)
+        return jnp.dot(pooled[rows, pl.ds(pl.multiple_of(p * depth, 128), depth)], w, preferred_element_type=F32)
+
+    def early(e, h):
+        for n in (2 * h, 2 * h + 1):
+            partial[e, :, 256 * n : 256 * n + 256] = plane_sum(e, 0, n, slice(None))
+
     def layer_one(e, h, rows=slice(None)):
         for n in (2 * h, 2 * h + 1):
             cols = slice(256 * n, 256 * n + 256)
-            w = w1[e, :, :, :, :, cols].reshape(16 * 208, 256)
-            summed = jnp.dot(pooled[rows], w, preferred_element_type=F32)
+            summed = partial[e, rows, cols] + plane_sum(e, 1, n, rows)
             first[rows, cols] = jnp.maximum(summed, 0.0).astype(BF16)
 
     def layers_two_three(e, start=0, size=tokens):
@@ -399,89 +419,102 @@
     first_round(0)
     quad(2)
     first_round(1)
+    first_round(2)
+    first_done(0)
+    push(gate_slot, gate_hbm, gate.at[1], task_peer)
+    share(0, 0, (0,))
     quad(3)
-    first_round(2)
-    first_round(3)
-    first_done(0)
-    first_far(1)
     near(0, 0)
-    first_far(2)
-    first_far(3)
     first_done(1)
     near(1, 0)
+    far(0, 0)
+    gates(1)
+    share(0, 0, (1, -1))
+    first_round(3)
+    share(1, 0, (0,))
+    by_plane()
+    far(1, 0)
+    first_far(2)
+    far_done(0, 0)
+    z_done(0)
+    share(0, 0, (2,))
+    share_arrived(0, 0)
+    share(1, 0, (1, -1))
+    early(0, 0)
+    far_done(1, 0)
+    share(1, 0, (2,))
+    early(0, 1)
+    share(0, 1, (0,))
     first_done(2)
-    z_done(0)
-    push(gate_slot, gate_hbm, gate.at[1], task_peer)
+    share(2, 0, (0,))
     near(2, 0)
+    first_far(3)
+    share_arrived(1, 0)
+    early(1, 0)
+    early(1, 1)
+    z_done(1)
     far(0, 1)
-    far(1, 0)
-    share(1, 0, (1, -1))
-    z_done(1)
-    far(0, 0)
+    share(0, 1, (1, -1))
     far(2, 0)
     first_done(3)
-    share(0, 0, (1, -1))
+    share(1, 1, (0,))
+    far(1, 1)
+    near(3, 0)
+    share(2, 0, (1, -1))
+    share(1, 1, (1, -1))
+    z_done(2)
     far_done(0, 1)
-    share(0, 1, (0,))
-    share(2, 0, (0,))
-    far_done(1, 0)
-    far(1, 1)
-    z_done(2)
-    share(0, 1, (1, -1))
-    share(2, 1, (0,))
-    share(0, 0, (0,))
-    far_done(0, 0)
-    share(0, 0, (2,))
-    near(3, 0)
     share(0, 1, (2,))
-    gates(1)
-    share(2, 0, (1, -1))
-    share(1, 1, (0,))
-    share_arrived(0)
-    share(1, 0, (2,))
-    z_done(3)
+    share_arrived(0, 1)
+    compute(0, 0)
     far_done(2, 0)
     share(2, 0, (2,))
-    share(1, 1, (1, -1))
-    share(3, 1, (0,))
-    share(1, 0, (0,))
-    compute(0, 0)
-    share(3, 0, (0,))
+    compute(0, 1)
     far_done(1, 1)
     share(1, 1, (2,))
-    compute(0, 1)
     compute(0, 2)
+    share_arrived(2, 0)
+    early(2, 0)
+    z_done(3)
+    share_arrived(1, 1)
+    compute(1, 0)
+    far(3, 0)
+    compute(1, 1)
+    early(2, 1)
+    share(3, 0, (0,))
+    share(2, 1, (0,))
+    compute(1, 2)
     far(2, 1)
-    share_arrived(1)
-    compute(1, 0)
-    compute(1, 1)
+    share(2, 1, (1, -1))
     far_done(2, 1)
-    share(2, 1, (1, -1))
-    far(3, 0)
     share(2, 1, (2,))
-    compute(1, 2)
-    others(0)
+    share(3, 0, (1, -1))
+    share(3, 1, (0,))
+    share_arrived(2, 1)
     far(3, 1)
-    share_arrived(2)
-    share(3, 1, (1, -1))
     compute(2, 0)
-    share(3, 0, (1, -1))
+    compute(2, 1)
     far_done(3, 0)
     share(3, 0, (2,))
-    compute(2, 1)
+    compute(2, 2)
+    share(3, 1, (1, -1))
+    share_arrived(3, 0)
+    early(3, 0)
     far_done(3, 1)
     share(3, 1, (2,))
-    compute(2, 2)
-    share_arrived(3)
+    early(3, 1)
+    share_arrived(3, 1)
     compute(3, 0)
     compute(3, 1)
+    compute(3, 2)
+    others(0)
+    others(2)
     others(1)
-    others(2)
-    compute(3, 2)
+    for copy in sent[:-3]:
+        copy.wait_send()
     for i in range(3):
         finish(i)
-
-    for copy in sent:
+    for copy in sent[-3:]:
         copy.wait_send()
 
 
@@ -507,6 +540,7 @@
             pltpu.VMEM((2, experts, 4, width), BF16),
             pltpu.VMEM((tokens, 1024), BF16),
             pltpu.VMEM((tokens, 512), BF16),
+            pltpu.VMEM((experts, tokens, 1024), F32),
             pltpu.VMEM((2, experts, tokens, 256), BF16),
             pltpu.VMEM((2, tokens, 256), F32),
             pltpu.VMEM((2, tokens, 2 * experts), F32),

time: 114 us -> 113 us (level)
  no operation moved by 1% of the time
where the time goes in v7:
time: 113 us
  Pallas kernels  111 us (98%)
  local copies, waits for them, and re-layouts  1.29 us (1%)
    pallas_call x1, Pallas kernels, per_device(): pl.pallas_call(kernel, out_shape=jax.ShapeDtypeStruct((2, tokens), F32),...  111 us

profile of v7, /device:TPU:1, one launch (start us, length us, event | category | flops | bytes accessed | tf_op | source)
XLA Modules:
  0.0 112.6 jit_solution(8515971915642841552)
XLA Ops:
  0.0 111.3 %shard_map.73 = f32[2,768]{1,0:T(2,128)} custom-call(bf16[768,3328]{1,0:T(8,128)(2,1)} %pooled_hbm.1, bf16[4,4,3328]{2,1,0:T(4,128)(2,1)} %bitcast.4, bf16[52,4,1024]{2,1,0:T(4,128)(2,1)} %bitcast.3, bf16[4,16,512]{2,1,0:T(8,128)(2,1)} %second_hbm.1, bf16[4,8,256]{2,1,0:T(8,128)(2,1)} %third_hbm.1, bf16[2,256,128]{2,1,0:T(8,128)(2,1)} %hidden_ref.1, ...), custom_call_target="tpu_custom_call" | custom-call | tf_op jit(solution)/shard_map/pallas_call | solution.py:526
  111.3 1.3 %copy.9 = f32[768,2]{0,1:T(2,128)} copy(f32[768,2]{0,1:T(2,128)} %bitcast.5) | data formatting | bytes 12288

commit v8 on v7

--- a/solution.py
+++ b/solution.py
@@ -338,7 +338,10 @@
                 weights[side, rows, 2 * e : 2 * e + 2] = jnp.exp(own)
 
     chunk = tokens // 3
-    eo_slots = [[slot() for _ in range(3)] for _ in range(experts)]
+    even = [(i * chunk, chunk) for i in range(3)]
+    short = chunk // 2
+    chunks = [even] * (experts - 1) + [[(0, short), (short, chunk), (short + chunk, chunk), (short + 2 * chunk, short)]]
+    eo_slots = [[slot() for _ in pieces] for pieces in chunks]
     assert used[0] <= send_sem.shape[0], used[0]
 
     def add_up(o, e, rows=slice(None)):
@@ -390,10 +393,11 @@
             eo[0, e, rows] = jnp.maximum(summed, 0.0).astype(BF16)
 
     def compute(e, i):
-        rows = pl.ds(i * chunk, chunk)
+        start, size = chunks[e][i]
+        rows = pl.ds(start, size)
         for h in range(2):
             layer_one(e, h, rows)
-        layers_two_three(e, i * chunk, chunk)
+        layers_two_three(e, start, size)
         push(eo_slots[e][i], eo.at[0, e, rows], eo.at[1, e, rows], task_peer)
         add_up(0, e, rows)
 
@@ -403,7 +407,7 @@
         add_up(1, e)
 
     def finish(i):
-        rows = pl.ds(i * chunk, chunk)
+        rows = pl.ds(*chunks[experts - 1][i])
         arrived(eo_slots[experts - 1][i], eo.at[1, experts - 1, rows])
         add_up(1, experts - 1, rows)
         for k in range(2):
@@ -507,14 +511,15 @@
     compute(3, 0)
     compute(3, 1)
     compute(3, 2)
+    compute(3, 3)
     others(0)
     others(2)
     others(1)
-    for copy in sent[:-3]:
+    for copy in sent[:-4]:
         copy.wait_send()
-    for i in range(3):
+    for i in range(4):
         finish(i)
-    for copy in sent[-3:]:
+    for copy in sent[-4:]:
         copy.wait_send()
 
 

time: 113 us -> 112 us (level)
  no operation moved by 1% of the time
where the time goes in v8:
time: 112 us
  Pallas kernels  111 us (99%)
  local copies, waits for them, and re-layouts  1.29 us (1%)
    pallas_call x1, Pallas kernels, per_device(): pl.pallas_call(kernel, out_shape=jax.ShapeDtypeStruct((2, tokens), F32),...  111 us

profile of v8, /device:TPU:1, one launch (start us, length us, event | category | flops | bytes accessed | tf_op | source)
XLA Modules:
  0.0 111.9 jit_solution(16351696936974682346)
XLA Ops:
  0.0 110.6 %shard_map.73 = f32[2,768]{1,0:T(2,128)} custom-call(bf16[768,3328]{1,0:T(8,128)(2,1)} %pooled_hbm.1, bf16[4,4,3328]{2,1,0:T(4,128)(2,1)} %bitcast.4, bf16[52,4,1024]{2,1,0:T(4,128)(2,1)} %bitcast.3, bf16[4,16,512]{2,1,0:T(8,128)(2,1)} %second_hbm.1, bf16[4,8,256]{2,1,0:T(8,128)(2,1)} %third_hbm.1, bf16[2,256,128]{2,1,0:T(8,128)(2,1)} %hidden_ref.1, ...), custom_call_target="tpu_custom_call" | custom-call | tf_op jit(solution)/shard_map/pallas_call | solution.py:531
  110.6 1.3 %copy.9 = f32[768,2]{0,1:T(2,128)} copy(f32[768,2]{0,1:T(2,128)} %bitcast.5) | data formatting | bytes 12288
